TPU v7x, 256 devices: a whole 4x4x8 slice. The times are simulated.
256 devices in a mesh: comp: 32 (over z_lo, x, core), rows: 8 (over y, z_hi).
Axes of the slice: x: 4, y: 4, z: 8 (z_hi: 2, z_lo: 4; z = z_hi * 4 + z_lo), core: 2. Of those that a mesh axis runs over, the one named last changes fastest.
Arguments:
- hidden_states: bfloat16 [8, 2, 32, 128, 2560], P('rows', None, 'comp'), may hold values from -6 to 6
- queries: bfloat16 [8, 2, 32, 128, 1280], P('rows', None, 'comp'), may hold values from -900 to 900
- new_keys: bfloat16 [8, 2, 32, 128, 1280], P('rows', None, 'comp'), may hold values from -6 to 6
- new_values: bfloat16 [8, 2, 32, 128, 1280], P('rows', None, 'comp'), may hold values from -6 to 6
- out_grad: bfloat16 [8, 2, 32, 128, 1280], P('rows', None, 'comp'), may hold values from -6 to 6
- gate_weight: bfloat16 [2560, 128], replicated, may hold values from -0.125 to 0.125
- gate_bias: float32 [128], replicated, may hold values from -2 to 6
- prompt_state: float32 [8, 32, 2, 2, 2, 64, 640], P('rows', 'comp'), may hold values from -6 to 6
- owners: int32 [8, 2], P('rows'), may hold values from 0 to 31
- lengths: int32 [8, 2, 32], P('rows', None, 'comp'), may hold values from 32 to 128
- advantage: float32 [8, 2, 32], P('rows', None, 'comp'), may hold values from -4 to 4
Outputs:
- d_queries: bfloat16 [8, 2, 32, 128, 1280], P('rows', None, 'comp')
- d_keys: bfloat16 [8, 2, 32, 128, 1280], P('rows', None, 'comp')
- d_values: bfloat16 [8, 2, 32, 128, 1280], P('rows', None, 'comp')
- d_hidden: bfloat16 [8, 2, 32, 128, 2560], P('rows', None, 'comp')
- d_gate_weight: float32 [2560, 128], replicated
- d_gate_bias: float32 [128], replicated
- d_state: float32 [8, 2, 2, 2, 64, 640], P('rows', None, None, None, 'comp')
All inputs are finite; a program needn't handle non-finite values.
Results may differ from a plain program's by a relative error of at most 0.011.
Values sent between devices are 32-bit elements; how exact they have to be, the bound alone decides.
No kernel may reach another device: no remote copies, remote signals or barrier semaphores. Data moves between devices by JAX's collectives and lax.ppermute only.
A program may use at most 64 MiB of HBM per device.

v0:
```python
import functools

import jax
import jax.numpy as jnp
from jax import lax
from jax.experimental import pallas as pl
from jax.experimental.pallas import tpu as pltpu
from jax.sharding import Mesh
from jax.sharding import PartitionSpec as P


F32 = jnp.float32
BF16 = jnp.bfloat16
D = 2560
T = 128
HM = 128
DH = 640
LEVELS = (64, 32, 16, 8, 4, 2, 1)
SCALE = DH ** (-0.5)
WROWS = 1280
BROWS = 8


def split2(x):
    high = x.astype(BF16)
    return high, (x - high.astype(F32)).astype(BF16)


def split3(x):
    high = x.astype(BF16)
    rest = x - high.astype(F32)
    middle = rest.astype(BF16)
    return high, middle, (rest - middle.astype(F32)).astype(BF16)


def mm(a, b):
    return jnp.dot(a, b, preferred_element_type=F32)


def mm_nt(a, b):
    return lax.dot_general(a, b, (((1,), (1,)), ((), ())), preferred_element_type=F32)


def mm_tn(a, b):
    return lax.dot_general(a, b, (((0,), (0,)), ((), ())), preferred_element_type=F32)


def mask_matmul(mask, x):
    high, middle, low = split3(x)
    return mm(mask, high) + mm(mask, middle) + mm(mask, low)


def iota(dim, shape):
    return lax.broadcasted_iota(jnp.int32, shape, dim)


def one_where(condition):
    return jnp.where(condition, 1.0, 0.0).astype(BF16)


def same_block(size, rows, cols):
    shift = size.bit_length() - 1
    row = jnp.right_shift(jnp.bitwise_and(iota(0, (rows, cols)), T - 1), shift)
    col = jnp.right_shift(jnp.bitwise_and(iota(1, (rows, cols)), T - 1), shift)
    return row == col


def odd_half(size):
    return jnp.bitwise_and(iota(0, (T, HM)), size) != 0


def pick_kernel(owners, states, keep, send, buffer, sems):
    core, x, z = lax.axis_index("c"), lax.axis_index("x"), lax.axis_index("z")
    index = (z * 4 + x) * 2 + core
    copies = [
        pltpu.make_async_copy(states.at[jnp.bitwise_xor(core, turn)], buffer.at[turn], sems.at[turn])
        for turn in (0, 1)
    ]
    copies[1].start()
    copies[0].start()
    for turn, out in ((1, send), (0, keep)):
        owned = owners[0, jnp.bitwise_xor(core, turn)] == index
        copies[turn].wait()
        for kx in range(4):
            for kz in range(4):
                row = jnp.bitwise_xor(z, kz) * 16
                block = buffer[turn, jnp.bitwise_xor(x, kx), pl.ds(pl.multiple_of(row, 16), 16), :]
                out[kx, kz] = jnp.where(owned, block, 0.0)


def first_kernel(turn, place, adv, hid, q, k, v, og, wg, bias, vec, at, yz):
    prompt = jnp.bitwise_xor(place[0], turn)
    length = place[6 + prompt]
    weight = adv[prompt]
    gates = mm(hid[0], wg[...]) + bias[...]
    u = jnp.exp(-jnp.abs(gates))
    s = u / (2.0 + u)
    s2 = s * s
    series = 1.0 / 17.0
    for n in (15, 13, 11, 9, 7, 5, 3, 1):
        series = series * s2 + 1.0 / n
    log1p = 2.0 * s * series
    log_keep = (jnp.minimum(gates, 0.0) - log1p) * 0.125
    keep = jnp.exp(log_keep)
    near = 1.0 + log_keep * (1.0 / 8.0)
    for n in (7, 6, 5, 4, 3, 2):
        near = 1.0 + log_keep * (1.0 / n) * near
    inflow = jnp.where(log_keep > -0.3, -log_keep * near, 1.0 - keep)
    slope = jnp.where(gates >= 0.0, u, 1.0) / (1.0 + u) * 0.125
    row = iota(0, (T, T))
    col = iota(1, (T, T))
    running = mask_matmul(one_where(col <= row), log_keep)
    vec[0, 0] = jnp.exp(running)
    vec[0, 1] = inflow
    vec[0, 2] = keep
    vec[0, 3] = slope

    live_col = jnp.where(iota(0, (T, 1)) < length, weight, 0.0)
    live_row = jnp.where(iota(1, (1, T)) < length, weight, 0.0)
    pairs, grads = [], []
    for h in range(2):
        cols = slice(h * DH, (h + 1) * DH)
        qh, kh, vh, gh = q[0, :, cols], k[0, :, cols], v[0, :, cols], og[0, :, cols]
        pairs.append(mm_nt(qh, kh) * SCALE)
        grads.append(mm_nt(gh, vh) * live_col)
        at[0, h * T : (h + 1) * T, 0:T] = mm_nt(kh, qh) * SCALE
        at[0, h * T : (h + 1) * T, T : 2 * T] = mm_nt(vh, gh) * live_row
    pairs = jnp.concatenate(pairs, axis=1)
    grads = jnp.concatenate(grads, axis=1)
    head0 = iota(1, (T, HM)) < 64
    grads_high, grads_low = split2(grads)

    def level(y, z, block):
        zs = jnp.concatenate([jnp.where(head0, z, 0.0), jnp.where(head0, 0.0, z)], axis=0)
        zs_high, zs_low = split2(zs)
        same = same_block(block, T, 2 * T)
        score = jnp.dot(jnp.where(same, pairs, 0.0), zs, precision=lax.Precision.HIGHEST, preferred_element_type=F32)
        gh = jnp.where(same, grads_high.astype(F32), 0.0).astype(BF16)
        gl = jnp.where(same, grads_low.astype(F32), 0.0).astype(BF16)
        grad = mm(gh, zs_high) + mm(gl, zs_high) + mm(gh, zs_low)
        if y is None:
            return score, grad
        return y * score, y * grad

    s1, t1 = level(None, inflow, 1)
    for n, size in enumerate(LEVELS):
        start = jnp.bitwise_and(row, -size)
        odd = jnp.bitwise_and(row, size) != 0
        low = jnp.where(odd, start, row + 1)
        high = jnp.where(odd, row, start + size - 1)
        decay = jnp.exp(mask_matmul(one_where((col >= low) & (col <= high)), log_keep))
        yz[0, n] = decay
        odd = odd_half(size)
        score, grad = level(jnp.where(odd, decay, 0.0), jnp.where(odd, 0.0, decay * inflow), 2 * size)
        s1 = s1 + score
        t1 = t1 + grad
    vec[0, 4] = s1
    vec[0, 5] = t1


def second_kernel(turn, place, adv, vec, at, yz, hid, q, og, anchors, *refs):
    core, x, z, y = place[0], place[1], place[2], place[3]
    prompt = jnp.bitwise_xor(core, turn)
    length = place[6 + prompt]
    weight = adv[prompt]
    hid_here, sem = refs[-2:]
    fetch = pltpu.make_async_copy(hid.at[prompt], hid_here, sem)
    fetch.start()
    if turn == 0:
        pd, dgl, kz_out, acc, bacc, kv = refs[:-2]
    else:
        acc_in, bacc_in, pd, dgl, kz_out, dw_keep, dw_send, acc, kv = refs[:-2]
    for i in range(4):
        for j in range(4):
            kv[i, j * 16 : (j + 1) * 16, :] = anchors[jnp.bitwise_xor(x, i), jnp.bitwise_xor(z, j)]

    live_col = jnp.where(iota(0, (T, 1)) < length, weight, 0.0)
    carried = vec[0, 0]
    inflow = vec[0, 1]
    keep = vec[0, 2]
    slope = vec[0, 3]
    head0 = iota(1, (T, HM)) < 64
    anchor_score, anchor_grad = [], []
    for h in range(2):
        cols = slice(h * DH, (h + 1) * DH)
        qh, gh = q[0, :, cols], og[0, :, cols]
        a, b, c = split3(kv[h])
        kz_out[h * 64 : (h + 1) * 64, :] = a
        anchor_score.append(mm_nt(qh, a) + mm_nt(qh, b) + mm_nt(qh, c))
        a, b = split2(kv[2 + h])
        anchor_grad.append(mm_nt(gh, a) + mm_nt(gh, b))
    anchor_score = jnp.concatenate(anchor_score, axis=1) * SCALE
    anchor_grad = jnp.concatenate(anchor_grad, axis=1) * live_col
    scores = vec[0, 4] + carried * anchor_score
    top0 = jnp.max(jnp.where(head0, scores, -jnp.inf), axis=1, keepdims=True)
    top1 = jnp.max(jnp.where(head0, -jnp.inf, scores), axis=1, keepdims=True)
    e = jnp.exp(scores - jnp.where(head0, top0, top1))
    sum0 = jnp.sum(jnp.where(head0, e, 0.0), axis=1, keepdims=True)
    sum1 = jnp.sum(jnp.where(head0, 0.0, e), axis=1, keepdims=True)
    probs = e / jnp.where(head0, sum0, sum1)
    d_probs = vec[0, 5] + carried * anchor_grad
    weighted = probs * d_probs
    dot0 = jnp.sum(jnp.where(head0, weighted, 0.0), axis=1, keepdims=True)
    dot1 = jnp.sum(jnp.where(head0, 0.0, weighted), axis=1, keepdims=True)
    d_scores = probs * (d_probs - jnp.where(head0, dot0, dot1))
    pd[0] = probs
    pd[1] = d_scores

    at_high, at_low = split2(at[0])
    at_high, at_low = at_high.astype(F32), at_low.astype(F32)

    def level(left, block):
        high, low = split2(left)
        same = same_block(block, 2 * T, 2 * T)
        ah = jnp.where(same, at_high, 0.0).astype(BF16)
        al = jnp.where(same, at_low, 0.0).astype(BF16)
        out = mm(ah, high) + mm(al, high) + mm(ah, low)
        return jnp.where(head0, out[0:T], out[T : 2 * T])

    both = jnp.concatenate([d_scores, probs], axis=0)
    held = level(both, 1)
    for n, size in enumerate(LEVELS):
        decay = yz[0, n]
        odd = odd_half(size)
        later = jnp.where(odd, decay, 0.0)
        earlier = jnp.where(odd, 0.0, decay)
        held = held + earlier * level(both * jnp.concatenate([later, later], axis=0), 2 * size)
    change = d_scores * scores + probs * d_probs - held * inflow
    row = iota(0, (T, T))
    col = iota(1, (T, T))
    d_log_keep = mask_matmul(one_where(col >= row), change) - held * keep
    d_gates = d_log_keep * slope
    low_gates = d_gates.astype(BF16)
    dgl[...] = low_gates
    bias = jnp.sum(d_gates, axis=0, keepdims=True)

    fetch.wait()
    update = mm_tn(hid_here[...], low_gates)
    if turn == 0:
        acc[...] = update
        bacc[...] = jnp.broadcast_to(bias, (BROWS, HM))
        return
    acc[...] = acc_in[...] + update
    total = bacc_in[...] + bias
    for kc, out in ((0, dw_keep), (1, dw_send)):
        out[WROWS : WROWS + BROWS, :] = total
        for ky in range(4):
            for kx in range(4):
                block = jnp.bitwise_xor(core, kc) * 16 + jnp.bitwise_xor(y, ky) * 4 + jnp.bitwise_xor(x, kx)
                start = (ky * 4 + kx) * 80
                out[start : start + 80, :] = acc[pl.ds(pl.multiple_of(block * 80, 8), 80), :]


def state_kernel(place, adv, vec_a, vec_b, pd_a, pd_b, q, og, ds_keep, ds_send):
    core, x, z = place[0], place[1], place[2]
    order = iota(0, (HM, HM))
    slot = iota(1, (HM, HM))
    place_c = jnp.bitwise_xor(jnp.bitwise_and(jnp.right_shift(order, 6), 1), core)
    place_x = jnp.bitwise_xor(jnp.bitwise_and(jnp.right_shift(order, 4), 3), x)
    place_z = jnp.bitwise_xor(jnp.bitwise_and(jnp.right_shift(order, 2), 3), z)
    head = jnp.bitwise_and(jnp.right_shift(order, 1), 1)
    wanted = head * 64 + place_z * 16 + place_x * 4 + place_c * 2 + jnp.bitwise_and(order, 1)
    move = one_where(slot == wanted)
    first_head = head == 0
    for turn, vec, pd in ((0, vec_a, pd_a), (1, vec_b, pd_b)):
        prompt = jnp.bitwise_xor(core, turn)
        live_col = jnp.where(iota(0, (T, 1)) < place[6 + prompt], adv[prompt], 0.0)
        carried = vec[0, 0]
        for kind, term in enumerate((pd[1] * carried * SCALE, pd[0] * carried * live_col)):
            data = (q, og)[kind]
            total = 0.0
            for part in split2(term):
                moved = mm_nt(move, part)
                for h in range(2):
                    left = jnp.where(first_head, moved, 0.0) if h == 0 else jnp.where(first_head, 0.0, moved)
                    total = total + mm(left.astype(BF16), data[prompt, :, h * DH : (h + 1) * DH])
            rows = slice(kind * 4, kind * 4 + 4)
            for kc, out in ((0, ds_keep), (1, ds_send)):
                for kx in range(4):
                    for kz in range(4):
                        start = kc * 64 + kx * 16 + kz * 4
                        for lane in range(5):
                            out[kx, kz, prompt, lane, rows, :] = total[start : start + 4, lane * 128 : lane * 128 + 128]


def third_kernel(turn, place, adv, vec, yz, pd, dgl, k0, q, k, og, wg, *refs):
    dq, dk, dv, dx = refs[-4:]
    prompt = jnp.bitwise_xor(place[0], turn)
    length = place[6 + prompt]
    weight = adv[prompt]
    live_col = jnp.where(iota(0, (T, 1)) < length, weight, 0.0)
    dx[0] = mm_nt(dgl[...], wg[...]).astype(BF16)
    inflow = vec[0, 1]
    probs = pd[0]
    d_scores = pd[1]
    head0 = iota(1, (T, HM)) < 64
    both = jnp.concatenate([probs, d_scores], axis=0)

    def level(left, right, block):
        zs = jnp.concatenate([jnp.where(head0, right, 0.0), jnp.where(head0, 0.0, right)], axis=0)
        zh, zl = split2(zs)
        lh, ll = split2(left)
        out = mm_nt(lh, zh) + mm_nt(ll, zh) + mm_nt(lh, zl)
        return jnp.where(same_block(block, 2 * T, 2 * T), out, 0.0)

    mix = level(both, inflow, 1)
    for n, size in enumerate(LEVELS):
        decay = yz[0, n]
        odd = odd_half(size)
        later = jnp.where(odd, decay, 0.0)
        earlier = jnp.where(odd, 0.0, decay * inflow)
        mix = mix + level(both * jnp.concatenate([later, later], axis=0), earlier, 2 * size)
    d_anchor = (d_scores * vec[0, 0]).astype(BF16)
    for h in range(2):
        cols = slice(h * DH, (h + 1) * DH)
        qh, kh, gh = q[0, :, cols], k[0, :, cols], og[0, :, cols]
        mixing = mix[0:T, h * T : (h + 1) * T].astype(BF16).astype(F32)
        d_pairs = mix[T : 2 * T, h * T : (h + 1) * T].astype(BF16)
        from_anchor = mm(d_anchor[:, h * 64 : (h + 1) * 64], k0[h * 64 : (h + 1) * 64, :])
        dq[0, :, cols] = ((mm(d_pairs, kh) + from_anchor) * SCALE).astype(BF16)
        dk[0, :, cols] = (mm_tn(d_pairs, qh) * SCALE).astype(BF16)
        dv[0, :, cols] = mm_tn((mixing * live_col).astype(BF16), gh).astype(BF16)


def place_kernel(half, source, *refs):
    out, sem = refs[-2:]
    core, x, y = lax.axis_index("c"), lax.axis_index("x"), lax.axis_index("y")
    copies = []
    for ky in range(4):
        for kx in range(4):
            block = jnp.bitwise_xor(core, half) * 16 + jnp.bitwise_xor(y, ky) * 4 + jnp.bitwise_xor(x, kx)
            here = out.at[pl.ds(pl.multiple_of(block * 80, 8), 80), :]
            copies.append(pltpu.make_async_copy(source.at[ky, kx], here, sem.at[ky, kx]))
            copies[-1].start()
    for copy in copies:
        copy.wait()


SMEM = pltpu.SMEM
VMEM = pltpu.VMEM


def whole(memory=VMEM):
    return pl.BlockSpec(memory_space=memory)


def fixed(shape):
    return pl.BlockSpec(shape, lambda i, *_: (0,) * len(shape))


def of_prompt(turn, shape):
    return pl.BlockSpec((1,) + shape, lambda i, place, *_: (jnp.bitwise_xor(place[0], turn),) + (0,) * len(shape))


def swap(value, axis, mask):
    count = 1
    for name in axis if isinstance(axis, tuple) else (axis,):
        count *= lax.axis_size(name)
    return lax.ppermute(value, axis, [(i, i ^ mask) for i in range(count)])


def exchange(values, axis):
    out = [values[0]]
    for i in (1, 2, 3):
        out.append(swap(values[i], axis, i))
    return out


def tree_sum(parts):
    while len(parts) > 1:
        parts = [parts[i] + parts[i + 1] for i in range(0, len(parts), 2)]
    return parts[0]


def struct(shape, dtype=F32):
    return jax.ShapeDtypeStruct(shape, dtype)


LIMIT = pltpu.CompilerParams(vmem_limit_bytes=24 * 1024 * 1024)


def local(value):
    return pltpu.with_memory_space_constraint(value, VMEM)


def call(kernel, in_specs, out_specs, out_shape, args, flops, aliases=None, scratch=()):
    return pl.pallas_call(
        kernel,
        grid_spec=pltpu.PrefetchScalarGridSpec(
            num_scalar_prefetch=2, grid=(1,), in_specs=in_specs, out_specs=out_specs, scratch_shapes=scratch
        ),
        out_shape=out_shape,
        input_output_aliases=aliases or {},
        cost_estimate=pl.CostEstimate(flops=int(flops), bytes_accessed=int(3e6), transcendentals=0),
        compiler_params=LIMIT,
    )(*args)


def program(hid, q, k, v, og, wg, bias, prompt_state, owners, lengths, advantage):
    hid, q, k, v, og = (a.reshape(2, T, a.shape[-1]) for a in (hid, q, k, v, og))
    states = prompt_state.reshape(2, 4, 64, DH)
    bias = bias.reshape(1, HM)
    core, x, z, y = (lax.axis_index(n) for n in ("c", "x", "z", "y"))
    zero = jnp.zeros((2,), jnp.int32)
    place = jnp.concatenate([jnp.stack([core, x, z, y]).astype(jnp.int32), zero, lengths.reshape(2)])
    adv = advantage.reshape(2)
    wide = (T, 2 * DH)

    keep, send = pl.pallas_call(
        pick_kernel,
        out_shape=(VMEM((4, 4, 16, DH), F32), VMEM((4, 4, 16, DH), F32)),
        in_specs=[whole(SMEM), whole(pl.ANY)],
        out_specs=(whole(), whole()),
        scratch_shapes=[VMEM((2, 4, 64, DH), F32), pltpu.SemaphoreType.DMA((2,))],
        compiler_params=LIMIT,
        name="pick",
    )(owners, states)

    other = swap(send, "c", 1)
    held = keep + other
    held = tree_sum(exchange([held[i] for i in range(4)], "x"))
    piece = tree_sum(exchange([held[i] for i in range(4)], "z"))
    column = jnp.stack(exchange([piece] * 4, "z"))
    mine = jnp.stack(exchange([column] * 4, "x"))
    other = swap(mine, "c", 1)

    def first(turn):
        return call(
            functools.partial(first_kernel, turn),
            [of_prompt(turn, (T, D))] + [of_prompt(turn, wide)] * 4 + [fixed((D, HM)), fixed((1, HM))],
            (whole(),) * 3,
            (VMEM((1, 6, T, HM), F32), VMEM((1, 2 * T, 2 * T), F32), VMEM((1, 7, T, HM), F32)),
            (place, adv, hid, q, k, v, og, wg, bias),
            3e9,
        )

    def second(turn, early, anchors, extra):
        kv = VMEM((4, 64, DH), F32)
        shapes = (VMEM((2, T, HM), F32), VMEM((T, HM), BF16), VMEM((HM, DH), BF16))
        if turn == 0:
            shapes += (VMEM((D, HM), F32), VMEM((BROWS, HM), F32))
            scratch = [kv]
        else:
            shapes += (VMEM((WROWS + BROWS, HM), F32),) * 2
            scratch = [VMEM((D, HM), F32), kv]
        return call(
            functools.partial(second_kernel, turn),
            [whole()] * 3
            + [whole(pl.ANY), of_prompt(turn, wide), of_prompt(turn, wide), whole()]
            + [whole()] * len(extra),
            (whole(),) * 5,
            shapes,
            (place, adv) + early + (hid, q, og, local(anchors)) + extra,
            3e9,
            scratch=scratch + [VMEM((T, D), BF16), pltpu.SemaphoreType.DMA],
        )

    early_a = tuple(local(a) for a in first(0))
    early_b = tuple(local(a) for a in first(1))
    pd_a, dgl_a, k0_a, acc, bacc = (local(a) for a in second(0, early_a, mine, ()))
    pd_b, dgl_b, k0_b, dw_keep, dw_send = second(1, early_b, other, (acc, bacc))
    pd_b, dgl_b, k0_b = local(pd_b), local(dgl_b), local(k0_b)

    ds_shape = (4, 4, 2, 5, 8, 128)
    ds_keep, ds_send = call(
        state_kernel,
        [whole()] * 4 + [fixed((2,) + wide), fixed((2,) + wide)],
        (whole(),) * 2,
        (VMEM(ds_shape, F32),) * 2,
        (place, adv, early_a[0], early_b[0], pd_a, pd_b, q, og),
        1e9,
    )

    other = swap(dw_send, "c", 1)
    held = dw_keep + other
    tail = held[1280:]
    held = tree_sum(exchange([jnp.concatenate([held[i * 320 : i * 320 + 320], tail]) for i in range(4)], "y"))
    tail = held[320:]
    arrived = swap(ds_send, "c", 1)
    states = (ds_keep + arrived).reshape(4, 320, 128)
    held = tree_sum(exchange([jnp.concatenate([held[i * 80 : i * 80 + 80], tail, states[i]]) for i in range(4)], "x"))
    tail = held[:88]
    held = tree_sum(exchange([jnp.concatenate([tail, held[88 + i * 80 : 168 + i * 80]]) for i in range(4)], "z"))
    d_state = held[88:].reshape(2, 5, 2, 2, 2, 128).transpose(0, 2, 3, 4, 1, 5).reshape(2, 2, 2, 2, DH)
    held = held[:88]
    held = held + swap(held, ("z", "zh"), 7)
    d_bias = held[80]
    piece = held[:80]
    line = jnp.stack(exchange([piece] * 4, "x"))
    mine = jnp.stack(exchange([line] * 4, "y"))
    other = swap(mine, "c", 1)

    def third(turn, early, pd, dgl, k0, earlier):
        return call(
            functools.partial(third_kernel, turn),
            [whole()] * 5
            + [of_prompt(turn, wide)] * 3
            + [fixed((D, HM))]
            + [whole(pl.ANY)] * len(earlier),
            (of_prompt(turn, wide),) * 3 + (of_prompt(turn, (T, D)),),
            (struct((2,) + wide, BF16),) * 3 + (struct((2, T, D), BF16),),
            (place, adv, early[0], early[2], pd, dgl, k0, q, k, og, wg) + earlier,
            3e9,
            aliases={11 + i: i for i in range(len(earlier))},
        )

    outs = third(0, early_a, pd_a, dgl_a, k0_a, ())
    outs = third(1, early_b, pd_b, dgl_b, k0_b, tuple(outs))

    def put(half, source, earlier):
        return pl.pallas_call(
            functools.partial(place_kernel, half),
            out_shape=struct((D, HM)),
            in_specs=[whole()] + [whole(pl.ANY)] * len(earlier),
            out_specs=whole(pl.ANY),
            input_output_aliases={1: 0} if earlier else {},
            scratch_shapes=[pltpu.SemaphoreType.DMA((4, 4))],
            compiler_params=LIMIT,
        )(local(source), *earlier)

    d_weight = put(1, other, (put(0, mine, ()),))

    dq, dk, dv, dx = (a.reshape(1, 2, 1, T, a.shape[-1]) for a in outs)
    return dq, dk, dv, dx, d_weight, d_bias, d_state[None]


def solution(mesh):
    fine = Mesh(mesh.devices.reshape(4, 4, 2, 4, 2), ("z", "x", "c", "y", "zh"))
    comp = ("z", "x", "c")
    rows = ("y", "zh")
    tokens = P(rows, None, comp, None, None)
    return jax.shard_map(
        program,
        mesh=fine,
        in_specs=(tokens,) * 5
        + (P(), P(), P(rows, comp, None, None, None, None, None), P(rows, None), P(rows, None, comp), P(rows, None, comp)),
        out_specs=(tokens,) * 4 + (P(), P(), P(rows, None, None, None, comp, None)),
        check_vma=False,
    )
```

profile of v0, /device:TPU:1, one launch (start us, length us, event | category | flops | bytes accessed | tf_op | source)
XLA Modules:
  0.0 141.1 jit_solution(2280693423258668868)
XLA Ops:
  0.6 1.3 copy-done
  2.0 0.7 copy-done.1
  2.6 1.2 pick.1
  3.8 3.3 %collective-permute-start = (f32[4,4,16,640]{3,2,1,0:T(8,128)S(1)}, f32[4,4,16,640]{3,2,1,0:T(8,128)S(1)}, u32[]{:S(2)}, u32[]{:S(2)}) collective-permute-start(f32[4,4,16,640]{3,2,1,0:T(8,128)S(1)} %get-tuple-element.39), channel_id=1, source_target_pairs={{0,8},{8,0},{1,9},{9,1},{2,10},{10,2},{3,11},{11,3},{4,12},{12,4},... | collective-permute-start | bytes 1966088 | tf_op jit(solution)/shard_map/ppermute | solution.py:359
  7.1 1.7 %collective-permute-done = f32[4,4,16,640]{3,2,1,0:T(8,128)S(1)} collective-permute-done((f32[4,4,16,640]{3,2,1,0:T(8,128)S(1)}, f32[4,4,16,640]{3,2,1,0:T(8,128)S(1)}, u32[]{:S(2)}, u32[]{:S(2)}) %collective-permute-start) | collective-permute-done | bytes 655392 | tf_op jit(solution)/shard_map/ppermute | solution.py:359
  8.9 0.9 collective-permute-start.3
  9.8 0.5 collective-permute-start.2
  10.3 2.0 %collective-permute-start.1 = (f32[4,16,640]{2,1,0:T(8,128)S(1)}, f32[4,16,640]{2,1,0:T(8,128)S(1)}, u32[]{:S(2)}, u32[]{:S(2)}) collective-permute-start(f32[4,16,640]{2,1,0:T(8,128)S(1)} %get-tuple-element.86), channel_id=1, source_target_pairs={{0,16},{16,0},{32,48},{48,32},{1,17},{17,1},{33,49},{49,33},{2,18}... | collective-permute-start | bytes 491528 | tf_op jit(solution)/shard_map/ppermute | solution.py:359
  12.3 6.9 %collective-permute-done.3 = f32[4,16,640]{2,1,0:T(8,128)S(1)} collective-permute-done((f32[4,16,640]{2,1,0:T(8,128)S(1)}, f32[4,16,640]{2,1,0:T(8,128)S(1)}, u32[]{:S(2)}, u32[]{:S(2)}) %collective-permute-start.3) | collective-permute-done | bytes 163872 | tf_op jit(solution)/shard_map/ppermute | solution.py:359
  19.6 2.7 %collective-permute-start.6 = (f32[16,640]{1,0:T(8,128)S(1)}, f32[16,640]{1,0:T(8,128)S(1)}, u32[]{:S(2)}, u32[]{:S(2)}) collective-permute-start(f32[16,640]{1,0:T(8,128)S(1)} %get-tuple-element.97), channel_id=1, source_target_pairs={{0,192},{64,128},{128,64},{192,0},{1,193},{65,129},{129,65},{193,1... | collective-permute-start | bytes 122888 | tf_op jit(solution)/shard_map/ppermute | solution.py:359
  22.4 0.9 collective-permute-start.4
  23.3 1.2 collective-permute-done.6
  24.5 2.4 %collective-permute-done.5 = f32[16,640]{1,0:T(8,128)S(1)} collective-permute-done((f32[16,640]{1,0:T(8,128)S(1)}, f32[16,640]{1,0:T(8,128)S(1)}, u32[]{:S(2)}, u32[]{:S(2)}) %collective-permute-start.5) | collective-permute-done | bytes 40992 | tf_op jit(solution)/shard_map/ppermute | solution.py:359
  26.9 1.2 collective-permute-start.9
  28.1 2.4 %collective-permute-start.7 = (f32[16,640]{1,0:T(8,128)S(1)}, f32[16,640]{1,0:T(8,128)S(1)}, u32[]{:S(2)}, u32[]{:S(2)}) collective-permute-start(f32[16,640]{1,0:T(8,128)S(1)} %fusion.11), channel_id=1, source_target_pairs={{0,64},{64,0},{128,192},{192,128},{1,65},{65,1},{129,193},{193,129... | collective-permute-start | bytes 122888 | tf_op jit(solution)/shard_map/ppermute | solution.py:359
  30.6 1.1 collective-permute-done.9
  31.7 1.2 collective-permute-done.8
  32.9 0.7 fusion.13
  33.6 1.7 %collective-permute-start.11 = (f32[4,16,640]{2,1,0:T(8,128)}, f32[4,16,640]{2,1,0:T(8,128)}, u32[]{:S(2)}, u32[]{:S(2)}) collective-permute-start(f32[4,16,640]{2,1,0:T(8,128)} %get-tuple-element.96), channel_id=1, source_target_pairs={{0,32},{16,48},{32,0},{48,16},{1,33},{17,49},{33,1},{49,17},{2,34}... | collective-permute-start | bytes 491528 | tf_op jit(solution)/shard_map/ppermute | solution.py:359
  35.6 1.3 collective-permute-start.12
  37.0 2.7 %collective-permute-done.11 = f32[4,16,640]{2,1,0:T(8,128)} collective-permute-done((f32[4,16,640]{2,1,0:T(8,128)}, f32[4,16,640]{2,1,0:T(8,128)}, u32[]{:S(2)}, u32[]{:S(2)}) %collective-permute-start.11) | collective-permute-done | bytes 163872 | tf_op jit(solution)/shard_map/ppermute | solution.py:359
  39.6 0.8 collective-permute-done.10
  40.4 1.0 collective-permute-done.12
  41.4 1.1 pad_maximum_fusion.anchors
  42.5 6.0 %collective-permute-start.13 = (f32[4,4,16,640]{3,2,1,0:T(8,128)S(1)}, f32[4,4,16,640]{3,2,1,0:T(8,128)S(1)}, u32[]{:S(2)}, u32[]{:S(2)}) collective-permute-start(f32[4,4,16,640]{3,2,1,0:T(8,128)S(1)} %pad_maximum_fusion.anchors), channel_id=1, source_target_pairs={{0,8},{8,0},{1,9},{9,1},{2,10},{10,2},{3,11},{11,3},{4,12},{12,4},... | collective-permute-start | bytes 1966088 | tf_op jit(solution)/shard_map/ppermute | solution.py:359
  48.5 1.1 copy-done.6
  49.6 1.1 copy-done.7
  50.7 4.2 %shard_map.163 = (f32[1,6,128,128]{3,2,1,0:T(8,128)S(1)}, f32[1,256,256]{2,1,0:T(8,128)S(1)}, f32[1,7,128,128]{3,2,1,0:T(8,128)S(1)}) custom-call(s32[8]{0:T(128)S(1)} %concatenate.40.place, f32[2]{0:T(128)S(1)} %bitcast.105, bf16[2,128,2560]{2,1,0:T(8,128)(2,1)S(1)} %bitcast.79, bf16[2,128,1280]{2,1,0:T(8,128)(2,1)S(1)} %bitcast.85, ...), custom_call_target="tpu_custom_call" | custom-call | flops 3000000000 | bytes 3000000 | tf_op jit(solution)/shard_map/pallas_call | solution.py:387
  54.8 4.2 %shard_map.162 = (f32[1,6,128,128]{3,2,1,0:T(8,128)S(1)}, f32[1,256,256]{2,1,0:T(8,128)S(1)}, f32[1,7,128,128]{3,2,1,0:T(8,128)S(1)}) custom-call(s32[8]{0:T(128)S(1)} %concatenate.40.place, f32[2]{0:T(128)S(1)} %bitcast.106, bf16[2,128,2560]{2,1,0:T(8,128)(2,1)S(1)} %bitcast.80, bf16[2,128,1280]{2,1,0:T(8,128)(2,1)S(1)} %bitcast.86, ...), custom_call_target="tpu_custom_call" | custom-call | flops 3000000000 | bytes 3000000 | tf_op jit(solution)/shard_map/pallas_call | solution.py:387
  59.0 3.2 %shard_map.164 = (f32[2,128,128]{2,1,0:T(8,128)S(1)}, bf16[128,128]{1,0:T(8,128)(2,1)S(1)}, bf16[128,640]{1,0:T(8,128)(2,1)S(1)}, f32[2560,128]{1,0:T(8,128)S(1)}, f32[8,128]{1,0:T(8,128)S(1)}) custom-call(s32[8]{0:T(128)S(1)} %concatenate.40.place, f32[2]{0:T(128)S(1)} %bitcast.107, f32[1,6,128,128]{3,2,1,0:T(8,128)S(1)} %get-tuple-element.40.vec.vec_a, ...), custom_call_target="tpu_custom_call" | custom-call | flops 3000000000 | bytes 3000000 | tf_op jit(solution)/shard_map/pallas_call | solution.py:387
  62.2 3.3 %shard_map.165 = (f32[2,128,128]{2,1,0:T(8,128)S(1)}, bf16[128,128]{1,0:T(8,128)(2,1)S(1)}, bf16[128,640]{1,0:T(8,128)(2,1)S(1)}, f32[1288,128]{1,0:T(8,128)S(1)}, f32[1288,128]{1,0:T(8,128)S(1)}) custom-call(s32[8]{0:T(128)S(1)} %concatenate.40.place, f32[2]{0:T(128)S(1)} %bitcast.108, f32[1,6,128,128]{3,2,1,0:T(8,128)S(1)} %get-tuple-element.35.vec.vec_b, ...), custom_call_target="tpu_custom_call" | custom-call | flops 3000000000 | bytes 3000000 | tf_op jit(solution)/shard_map/pallas_call | solution.py:387
  65.9 2.4 %shard_map.168 = (f32[4,4,2,5,8,128]{5,4,3,2,1,0:T(8,128)S(1)}, f32[4,4,2,5,8,128]{5,4,3,2,1,0:T(8,128)S(1)}) custom-call(s32[8]{0:T(128)S(1)} %concatenate.40.place, f32[2]{0:T(128)S(1)} %bitcast.109, f32[1,6,128,128]{3,2,1,0:T(8,128)S(1)} %get-tuple-element.40.vec.vec_a, f32[1,6,128,128]{3,2,1,0:T(8,128)S(1)} %get-tuple-element.35.vec.vec_b, ...), custom_call_target="tpu_custom_call" | custom-call | flops 1000000000 | bytes 3000000 | tf_op jit(solution)/shard_map/pallas_call | solution.py:387
  68.3 0.6 collective-permute-start.18
  68.9 1.7 %collective-permute-done.18 = f32[4,4,2,5,8,128]{5,4,3,2,1,0:T(8,128)S(1)} collective-permute-done((f32[4,4,2,5,8,128]{5,4,3,2,1,0:T(8,128)S(1)}, f32[4,4,2,5,8,128]{5,4,3,2,1,0:T(8,128)S(1)}, u32[]{:S(2)}, u32[]{:S(2)}) %collective-permute-start.18) | collective-permute-done | bytes 655392 | tf_op jit(solution)/shard_map/ppermute | solution.py:359
  70.9 3.0 %collective-permute-start.16 = (f32[328,128]{1,0:T(8,128)S(1)}, f32[328,128]{1,0:T(8,128)S(1)}, u32[]{:S(2)}, u32[]{:S(2)}) collective-permute-start(f32[328,128]{1,0:T(8,128)S(1)} %get-tuple-element.107), channel_id=1, source_target_pairs={{0,4},{2,6},{4,0},{6,2},{1,5},{3,7},{5,1},{7,3},{8,12},{10,14},{12... | collective-permute-start | bytes 503816 | tf_op jit(solution)/shard_map/ppermute | solution.py:359
  74.7 3.2 %collective-permute-done.16 = f32[328,128]{1,0:T(8,128)S(1)} collective-permute-done((f32[328,128]{1,0:T(8,128)S(1)}, f32[328,128]{1,0:T(8,128)S(1)}, u32[]{:S(2)}, u32[]{:S(2)}) %collective-permute-start.16) | collective-permute-done | bytes 167968 | tf_op jit(solution)/shard_map/ppermute | solution.py:359
  78.0 4.0 %collective-permute-done.15 = f32[328,128]{1,0:T(8,128)S(1)} collective-permute-done((f32[328,128]{1,0:T(8,128)S(1)}, f32[328,128]{1,0:T(8,128)S(1)}, u32[]{:S(2)}, u32[]{:S(2)}) %collective-permute-start.15) | collective-permute-done | bytes 167968 | tf_op jit(solution)/shard_map/ppermute | solution.py:359
  82.1 1.3 collective-permute-start.20
  83.7 1.8 %collective-permute-start.21 = (f32[408,128]{1,0:T(8,128)S(1)}, f32[408,128]{1,0:T(8,128)S(1)}, u32[]{:S(2)}, u32[]{:S(2)}) collective-permute-start(f32[408,128]{1,0:T(8,128)S(1)} %pad_maximum_fusion.8), channel_id=1, source_target_pairs={{0,48},{16,32},{32,16},{48,0},{1,49},{17,33},{33,17},{49,1},{2,50}... | collective-permute-start | bytes 626696 | tf_op jit(solution)/shard_map/ppermute | solution.py:359
  85.5 3.6 %collective-permute-done.20 = f32[408,128]{1,0:T(8,128)S(1)} collective-permute-done((f32[408,128]{1,0:T(8,128)S(1)}, f32[408,128]{1,0:T(8,128)S(1)}, u32[]{:S(2)}, u32[]{:S(2)}) %collective-permute-start.20) | collective-permute-done | bytes 208928 | tf_op jit(solution)/shard_map/ppermute | solution.py:359
  89.1 3.0 %collective-permute-done.19 = f32[408,128]{1,0:T(8,128)S(1)} collective-permute-done((f32[408,128]{1,0:T(8,128)S(1)}, f32[408,128]{1,0:T(8,128)S(1)}, u32[]{:S(2)}, u32[]{:S(2)}) %collective-permute-start.19) | collective-permute-done | bytes 208928 | tf_op jit(solution)/shard_map/ppermute | solution.py:359
  92.2 2.8 %collective-permute-done.21 = f32[408,128]{1,0:T(8,128)S(1)} collective-permute-done((f32[408,128]{1,0:T(8,128)S(1)}, f32[408,128]{1,0:T(8,128)S(1)}, u32[]{:S(2)}, u32[]{:S(2)}) %collective-permute-start.21) | collective-permute-done | bytes 208928 | tf_op jit(solution)/shard_map/ppermute | solution.py:359
  95.0 2.2 %collective-permute-start.24 = (f32[168,128]{1,0:T(8,128)S(1)}, f32[168,128]{1,0:T(8,128)S(1)}, u32[]{:S(2)}, u32[]{:S(2)}) collective-permute-start(f32[168,128]{1,0:T(8,128)S(1)} %get-tuple-element.102), channel_id=1, source_target_pairs={{0,192},{64,128},{128,64},{192,0},{1,193},{65,129},{129,65},{193,1... | collective-permute-start | bytes 258056 | tf_op jit(solution)/shard_map/ppermute | solution.py:359
  97.2 0.4 collective-permute-start.23
  97.6 1.0 collective-permute-start.22
  98.7 1.7 %collective-permute-done.24 = f32[168,128]{1,0:T(8,128)S(1)} collective-permute-done((f32[168,128]{1,0:T(8,128)S(1)}, f32[168,128]{1,0:T(8,128)S(1)}, u32[]{:S(2)}, u32[]{:S(2)}) %collective-permute-start.24) | collective-permute-done | bytes 86048 | tf_op jit(solution)/shard_map/ppermute | solution.py:359
  100.4 5.0 %collective-permute-done.23 = f32[168,128]{1,0:T(8,128)S(1)} collective-permute-done((f32[168,128]{1,0:T(8,128)S(1)}, f32[168,128]{1,0:T(8,128)S(1)}, u32[]{:S(2)}, u32[]{:S(2)}) %collective-permute-start.23) | collective-permute-done | bytes 86048 | tf_op jit(solution)/shard_map/ppermute | solution.py:359
  105.4 3.5 %collective-permute-start.25 = (f32[88,128]{1,0:T(8,128)S(1)}, f32[88,128]{1,0:T(8,128)S(1)}, u32[]{:S(2)}, u32[]{:S(2)}) collective-permute-start(f32[88,128]{1,0:T(8,128)S(1)} %slice.150), channel_id=1, source_target_pairs={{0,193},{1,192},{64,129},{65,128},{128,65},{129,64},{192,1},{193,0... | collective-permute-start | bytes 135176 | tf_op jit(solution)/shard_map/ppermute | solution.py:359
  108.9 1.4 %collective-permute-done.25 = f32[88,128]{1,0:T(8,128)S(1)} collective-permute-done((f32[88,128]{1,0:T(8,128)S(1)}, f32[88,128]{1,0:T(8,128)S(1)}, u32[]{:S(2)}, u32[]{:S(2)}) %collective-permute-start.25) | collective-permute-done | bytes 45088 | tf_op jit(solution)/shard_map/ppermute | solution.py:359
  110.4 1.4 %collective-permute-start.27 = (f32[80,128]{1,0:T(8,128)S(1)}, f32[80,128]{1,0:T(8,128)S(1)}, u32[]{:S(2)}, u32[]{:S(2)}) collective-permute-start(f32[80,128]{1,0:T(8,128)S(1)} %get-tuple-element.101), channel_id=1, source_target_pairs={{0,32},{16,48},{32,0},{48,16},{1,33},{17,49},{33,1},{49,17},{2,34}... | collective-permute-start | bytes 122888 | tf_op jit(solution)/shard_map/ppermute | solution.py:359
  111.8 1.9 %collective-permute-start.28 = (f32[80,128]{1,0:T(8,128)S(1)}, f32[80,128]{1,0:T(8,128)S(1)}, u32[]{:S(2)}, u32[]{:S(2)}) collective-permute-start(f32[80,128]{1,0:T(8,128)S(1)} %get-tuple-element.101), channel_id=1, source_target_pairs={{0,48},{16,32},{32,16},{48,0},{1,49},{17,33},{33,17},{49,1},{2,50}... | collective-permute-start | bytes 122888 | tf_op jit(solution)/shard_map/ppermute | solution.py:359
  113.7 1.1 collective-permute-done.27
  114.8 1.1 collective-permute-done.28
  115.9 3.8 %collective-permute-start.30 = (f32[4,80,128]{2,1,0:T(8,128)S(1)}, f32[4,80,128]{2,1,0:T(8,128)S(1)}, u32[]{:S(2)}, u32[]{:S(2)}) collective-permute-start(f32[4,80,128]{2,1,0:T(8,128)S(1)} %get-tuple-element.94), channel_id=1, source_target_pairs={{0,4},{2,6},{4,0},{6,2},{1,5},{3,7},{5,1},{7,3},{8,12},{10,14},{12... | collective-permute-start | bytes 491528 | tf_op jit(solution)/shard_map/ppermute | solution.py:359
  120.3 2.1 %collective-permute-done.30 = f32[4,80,128]{2,1,0:T(8,128)S(1)} collective-permute-done((f32[4,80,128]{2,1,0:T(8,128)S(1)}, f32[4,80,128]{2,1,0:T(8,128)S(1)}, u32[]{:S(2)}, u32[]{:S(2)}) %collective-permute-start.30) | collective-permute-done | bytes 163872 | tf_op jit(solution)/shard_map/ppermute | solution.py:359
  122.4 2.1 %collective-permute-done.29 = f32[4,80,128]{2,1,0:T(8,128)S(1)} collective-permute-done((f32[4,80,128]{2,1,0:T(8,128)S(1)}, f32[4,80,128]{2,1,0:T(8,128)S(1)}, u32[]{:S(2)}, u32[]{:S(2)}) %collective-permute-start.29) | collective-permute-done | bytes 163872 | tf_op jit(solution)/shard_map/ppermute | solution.py:359
  124.5 2.7 %collective-permute-done.31 = f32[4,80,128]{2,1,0:T(8,128)S(1)} collective-permute-done((f32[4,80,128]{2,1,0:T(8,128)S(1)}, f32[4,80,128]{2,1,0:T(8,128)S(1)}, u32[]{:S(2)}, u32[]{:S(2)}) %collective-permute-start.31) | collective-permute-done | bytes 163872 | tf_op jit(solution)/shard_map/ppermute | solution.py:359
  127.3 4.1 %collective-permute-start.32 = (f32[4,4,80,128]{3,2,1,0:T(8,128)S(1)}, f32[4,4,80,128]{3,2,1,0:T(8,128)S(1)}, u32[]{:S(2)}, u32[]{:S(2)}) collective-permute-start(f32[4,4,80,128]{3,2,1,0:T(8,128)S(1)} %pad_maximum_fusion.1.source), channel_id=1, source_target_pairs={{0,8},{8,0},{1,9},{9,1},{2,10},{10,2},{3,11},{11,3},{4,12},{12,4},... | collective-permute-start | bytes 1966088 | tf_op jit(solution)/shard_map/ppermute | solution.py:359
  131.3 3.2 %shard_map.166 = (bf16[2,128,1280]{2,1,0:T(8,128)(2,1)}, bf16[2,128,1280]{2,1,0:T(8,128)(2,1)}, bf16[2,128,1280]{2,1,0:T(8,128)(2,1)}, bf16[2,128,2560]{2,1,0:T(8,128)(2,1)}) custom-call(s32[8]{0:T(128)S(1)} %concatenate.40.place, f32[2]{0:T(128)S(1)} %bitcast.110, f32[1,6,128,128]{3,2,1,0:T(8,128)S(1)} %get-tuple-element.40.vec.vec_a, ...), custom_call_target="tpu_custom_call" | custom-call | flops 3000000000 | bytes 3000000 | tf_op jit(solution)/shard_map/pallas_call | solution.py:387
  134.6 3.2 %shard_map.167 = (bf16[2,128,1280]{2,1,0:T(8,128)(2,1)}, bf16[2,128,1280]{2,1,0:T(8,128)(2,1)}, bf16[2,128,1280]{2,1,0:T(8,128)(2,1)}, bf16[2,128,2560]{2,1,0:T(8,128)(2,1)}) custom-call(s32[8]{0:T(128)S(1)} %concatenate.40.place, f32[2]{0:T(128)S(1)} %bitcast.111, ...), custom_call_target="tpu_custom_call", output_to_operand_aliasing={{0}: (11, {}), {1}: (12, {}), {2}: (13, {}), {3}: (14, {})} | custom-call | flops 3000000000 | bytes 3000000 | tf_op jit(solution)/shard_map/pallas_call | solution.py:387
  137.8 0.6 broadcast_in_dim_reshape.3
  138.5 0.5 slice_bitcast_fusion.8
  139.0 1.0 shard_map.169.refs_0_
  140.0 1.0 shard_map.170
  (70 shorter events, 3.7 us)
Async XLA Ops:
  0.6 1.3 copy-start
  1.9 0.7 copy-start.1
  3.8 5.0 %collective-permute-start = (f32[4,4,16,640]{3,2,1,0:T(8,128)S(1)}, f32[4,4,16,640]{3,2,1,0:T(8,128)S(1)}, u32[]{:S(2)}, u32[]{:S(2)}) collective-permute-start(f32[4,4,16,640]{3,2,1,0:T(8,128)S(1)} %get-tuple-element.39), channel_id=1, source_target_pairs={{0,8},{8,0},{1,9},{9,1},{2,10},{10,2},{3,11},{11,3},{4,12},{12,4},... | collective-permute-start | bytes 1966088 | tf_op jit(solution)/shard_map/ppermute | solution.py:359
  8.9 28.0 %copy-start.10 = (s32[1,2,1]{1,2,0:T(1,128)S(1)}, s32[1,2,1]{1,2,0:T(1,128)}, u32[]{:S(2)}) copy-start(s32[1,2,1]{1,2,0:T(1,128)} %param.20) | copy-start | bytes 28
  8.9 39.6 %copy-start.5 = (bf16[1,2,1,128,1280]{4,3,2,1,0:T(8,128)(2,1)S(1)}, bf16[1,2,1,128,1280]{4,3,2,1,0:T(8,128)(2,1)}, u32[]{:S(2)}) copy-start(bf16[1,2,1,128,1280]{4,3,2,1,0:T(8,128)(2,1)} %param.13) | copy-start | bytes 1966084
  8.9 10.2 %collective-permute-start.3 = (f32[4,16,640]{2,1,0:T(8,128)S(1)}, f32[4,16,640]{2,1,0:T(8,128)S(1)}, u32[]{:S(2)}, u32[]{:S(2)}) collective-permute-start(f32[4,16,640]{2,1,0:T(8,128)S(1)} %get-tuple-element.84), channel_id=1, source_target_pairs={{0,48},{16,32},{32,16},{48,0},{1,49},{17,33},{33,17},{49,1},{2,50}... | collective-permute-start | bytes 491528 | tf_op jit(solution)/shard_map/ppermute | solution.py:359
  9.8 9.3 %collective-permute-start.2 = (f32[4,16,640]{2,1,0:T(8,128)S(1)}, f32[4,16,640]{2,1,0:T(8,128)S(1)}, u32[]{:S(2)}, u32[]{:S(2)}) collective-permute-start(f32[4,16,640]{2,1,0:T(8,128)S(1)} %get-tuple-element.85), channel_id=1, source_target_pairs={{0,32},{16,48},{32,0},{48,16},{1,33},{17,49},{33,1},{49,17},{2,34}... | collective-permute-start | bytes 491528 | tf_op jit(solution)/shard_map/ppermute | solution.py:359
  10.3 9.2 %collective-permute-start.1 = (f32[4,16,640]{2,1,0:T(8,128)S(1)}, f32[4,16,640]{2,1,0:T(8,128)S(1)}, u32[]{:S(2)}, u32[]{:S(2)}) collective-permute-start(f32[4,16,640]{2,1,0:T(8,128)S(1)} %get-tuple-element.86), channel_id=1, source_target_pairs={{0,16},{16,0},{32,48},{48,32},{1,17},{17,1},{33,49},{49,33},{2,18}... | collective-permute-start | bytes 491528 | tf_op jit(solution)/shard_map/ppermute | solution.py:359
  19.5 28.9 %copy-start.4 = (bf16[1,2,1,128,1280]{4,3,2,1,0:T(8,128)(2,1)S(1)}, bf16[1,2,1,128,1280]{4,3,2,1,0:T(8,128)(2,1)}, u32[]{:S(2)}) copy-start(bf16[1,2,1,128,1280]{4,3,2,1,0:T(8,128)(2,1)} %param.12) | copy-start | bytes 1966084
  19.6 28.9 %copy-start.2 = (bf16[1,2,1,128,2560]{4,3,2,1,0:T(8,128)(2,1)S(1)}, bf16[1,2,1,128,2560]{4,3,2,1,0:T(8,128)(2,1)}, u32[]{:S(2)}) copy-start(bf16[1,2,1,128,2560]{4,3,2,1,0:T(8,128)(2,1)} %param.11) | copy-start | bytes 3932164
  19.6 28.9 %copy-start.3 = (bf16[1,2,1,128,1280]{4,3,2,1,0:T(8,128)(2,1)S(1)}, bf16[1,2,1,128,1280]{4,3,2,1,0:T(8,128)(2,1)}, u32[]{:S(2)}) copy-start(bf16[1,2,1,128,1280]{4,3,2,1,0:T(8,128)(2,1)} %param.14) | copy-start | bytes 1966084
  19.6 28.9 %copy-start.8 = (f32[128]{0:T(128)S(1)}, f32[128]{0:T(128)}, u32[]{:S(2)}) copy-start(f32[128]{0:T(128)} %param.17) | copy-start | bytes 1540
  19.6 28.9 %copy-start.9 = (f32[1,2,1]{1,2,0:T(1,128)S(1)}, f32[1,2,1]{1,2,0:T(1,128)}, u32[]{:S(2)}) copy-start(f32[1,2,1]{1,2,0:T(1,128)} %param.21) | copy-start | bytes 28
  19.6 4.8 %collective-permute-start.6 = (f32[16,640]{1,0:T(8,128)S(1)}, f32[16,640]{1,0:T(8,128)S(1)}, u32[]{:S(2)}, u32[]{:S(2)}) collective-permute-start(f32[16,640]{1,0:T(8,128)S(1)} %get-tuple-element.97), channel_id=1, source_target_pairs={{0,192},{64,128},{128,64},{192,0},{1,193},{65,129},{129,65},{193,1... | collective-permute-start | bytes 122888 | tf_op jit(solution)/shard_map/ppermute | solution.py:359
  22.4 4.5 %collective-permute-start.5 = (f32[16,640]{1,0:T(8,128)S(1)}, f32[16,640]{1,0:T(8,128)S(1)}, u32[]{:S(2)}, u32[]{:S(2)}) collective-permute-start(f32[16,640]{1,0:T(8,128)S(1)} %get-tuple-element.98), channel_id=1, source_target_pairs={{0,128},{64,192},{128,0},{192,64},{1,129},{65,193},{129,1},{193,65... | collective-permute-start | bytes 122888 | tf_op jit(solution)/shard_map/ppermute | solution.py:359
  22.4 4.5 %collective-permute-start.4 = (f32[16,640]{1,0:T(8,128)S(1)}, f32[16,640]{1,0:T(8,128)S(1)}, u32[]{:S(2)}, u32[]{:S(2)}) collective-permute-start(f32[16,640]{1,0:T(8,128)S(1)} %get-tuple-element.99), channel_id=1, source_target_pairs={{0,64},{64,0},{128,192},{192,128},{1,65},{65,1},{129,193},{193,129... | collective-permute-start | bytes 122888 | tf_op jit(solution)/shard_map/ppermute | solution.py:359
  26.9 4.8 %collective-permute-start.9 = (f32[16,640]{1,0:T(8,128)S(1)}, f32[16,640]{1,0:T(8,128)S(1)}, u32[]{:S(2)}, u32[]{:S(2)}) collective-permute-start(f32[16,640]{1,0:T(8,128)S(1)} %fusion.11), channel_id=1, source_target_pairs={{0,192},{64,128},{128,64},{192,0},{1,193},{65,129},{129,65},{193,1... | collective-permute-start | bytes 122888 | tf_op jit(solution)/shard_map/ppermute | solution.py:359
  28.1 4.8 %collective-permute-start.8 = (f32[16,640]{1,0:T(8,128)S(1)}, f32[16,640]{1,0:T(8,128)S(1)}, u32[]{:S(2)}, u32[]{:S(2)}) collective-permute-start(f32[16,640]{1,0:T(8,128)S(1)} %fusion.11), channel_id=1, source_target_pairs={{0,128},{64,192},{128,0},{192,64},{1,129},{65,193},{129,1},{193,65... | collective-permute-start | bytes 122888 | tf_op jit(solution)/shard_map/ppermute | solution.py:359
  28.1 4.8 %collective-permute-start.7 = (f32[16,640]{1,0:T(8,128)S(1)}, f32[16,640]{1,0:T(8,128)S(1)}, u32[]{:S(2)}, u32[]{:S(2)}) collective-permute-start(f32[16,640]{1,0:T(8,128)S(1)} %fusion.11), channel_id=1, source_target_pairs={{0,64},{64,0},{128,192},{192,128},{1,65},{65,1},{129,193},{193,129... | collective-permute-start | bytes 122888 | tf_op jit(solution)/shard_map/ppermute | solution.py:359
  33.6 6.0 %collective-permute-start.11 = (f32[4,16,640]{2,1,0:T(8,128)}, f32[4,16,640]{2,1,0:T(8,128)}, u32[]{:S(2)}, u32[]{:S(2)}) collective-permute-start(f32[4,16,640]{2,1,0:T(8,128)} %get-tuple-element.96), channel_id=1, source_target_pairs={{0,32},{16,48},{32,0},{48,16},{1,33},{17,49},{33,1},{49,17},{2,34}... | collective-permute-start | bytes 491528 | tf_op jit(solution)/shard_map/ppermute | solution.py:359
  35.3 5.1 %collective-permute-start.10 = (f32[4,16,640]{2,1,0:T(8,128)}, f32[4,16,640]{2,1,0:T(8,128)}, u32[]{:S(2)}, u32[]{:S(2)}) collective-permute-start(f32[4,16,640]{2,1,0:T(8,128)} %get-tuple-element.96), channel_id=1, source_target_pairs={{0,16},{16,0},{32,48},{48,32},{1,17},{17,1},{33,49},{49,33},{2,18}... | collective-permute-start | bytes 491528 | tf_op jit(solution)/shard_map/ppermute | solution.py:359
  35.6 5.8 %collective-permute-start.12 = (f32[4,16,640]{2,1,0:T(8,128)}, f32[4,16,640]{2,1,0:T(8,128)}, u32[]{:S(2)}, u32[]{:S(2)}) collective-permute-start(f32[4,16,640]{2,1,0:T(8,128)} %get-tuple-element.96), channel_id=1, source_target_pairs={{0,48},{16,32},{32,16},{48,0},{1,49},{17,33},{33,17},{49,1},{2,50}... | collective-permute-start | bytes 491528 | tf_op jit(solution)/shard_map/ppermute | solution.py:359
  42.5 19.8 %collective-permute-start.13 = (f32[4,4,16,640]{3,2,1,0:T(8,128)S(1)}, f32[4,4,16,640]{3,2,1,0:T(8,128)S(1)}, u32[]{:S(2)}, u32[]{:S(2)}) collective-permute-start(f32[4,4,16,640]{3,2,1,0:T(8,128)S(1)} %pad_maximum_fusion.anchors), channel_id=1, source_target_pairs={{0,8},{8,0},{1,9},{9,1},{2,10},{10,2},{3,11},{11,3},{4,12},{12,4},... | collective-permute-start | bytes 1966088 | tf_op jit(solution)/shard_map/ppermute | solution.py:359
  48.5 1.1 copy-start.6
  49.6 1.1 copy-start.7
  65.6 5.1 %collective-permute-start.14 = (f32[1288,128]{1,0:T(8,128)S(1)}, f32[1288,128]{1,0:T(8,128)S(1)}, u32[]{:S(2)}, u32[]{:S(2)}) collective-permute-start(f32[1288,128]{1,0:T(8,128)S(1)} %get-tuple-element.60), channel_id=1, source_target_pairs={{0,8},{8,0},{1,9},{9,1},{2,10},{10,2},{3,11},{11,3},{4,12},{12,4},... | collective-permute-start | bytes 1978376 | tf_op jit(solution)/shard_map/ppermute | solution.py:359
  68.3 2.3 %collective-permute-start.18 = (f32[4,4,2,5,8,128]{5,4,3,2,1,0:T(8,128)S(1)}, f32[4,4,2,5,8,128]{5,4,3,2,1,0:T(8,128)S(1)}, u32[]{:S(2)}, u32[]{:S(2)}) collective-permute-start(f32[4,4,2,5,8,128]{5,4,3,2,1,0:T(8,128)S(1)} %get-tuple-element.62), channel_id=1, source_target_pairs={{0,8},{8,0},{1,9},{9,1},{2,10},{10,2},{3,11},{11,3},{4,12},{12,4},... | collective-permute-start | bytes 1966088 | tf_op jit(solution)/shard_map/ppermute | solution.py:359
  70.9 7.1 %collective-permute-start.16 = (f32[328,128]{1,0:T(8,128)S(1)}, f32[328,128]{1,0:T(8,128)S(1)}, u32[]{:S(2)}, u32[]{:S(2)}) collective-permute-start(f32[328,128]{1,0:T(8,128)S(1)} %get-tuple-element.107), channel_id=1, source_target_pairs={{0,4},{2,6},{4,0},{6,2},{1,5},{3,7},{5,1},{7,3},{8,12},{10,14},{12... | collective-permute-start | bytes 503816 | tf_op jit(solution)/shard_map/ppermute | solution.py:359
  73.9 8.0 %collective-permute-start.15 = (f32[328,128]{1,0:T(8,128)S(1)}, f32[328,128]{1,0:T(8,128)S(1)}, u32[]{:S(2)}, u32[]{:S(2)}) collective-permute-start(f32[328,128]{1,0:T(8,128)S(1)} %get-tuple-element.108), channel_id=1, source_target_pairs={{0,2},{2,0},{4,6},{6,4},{1,3},{3,1},{5,7},{7,5},{8,10},{10,8},{12,... | collective-permute-start | bytes 503816 | tf_op jit(solution)/shard_map/ppermute | solution.py:359
  74.3 7.7 %collective-permute-start.17 = (f32[328,128]{1,0:T(8,128)S(1)}, f32[328,128]{1,0:T(8,128)S(1)}, u32[]{:S(2)}, u32[]{:S(2)}) collective-permute-start(f32[328,128]{1,0:T(8,128)S(1)} %concatenate.53), channel_id=1, source_target_pairs={{0,6},{2,4},{4,2},{6,0},{1,7},{3,5},{5,3},{7,1},{8,14},{10,12},{12... | collective-permute-start | bytes 503816 | tf_op jit(solution)/shard_map/ppermute | solution.py:359
  82.1 7.1 %collective-permute-start.20 = (f32[408,128]{1,0:T(8,128)S(1)}, f32[408,128]{1,0:T(8,128)S(1)}, u32[]{:S(2)}, u32[]{:S(2)}) collective-permute-start(f32[408,128]{1,0:T(8,128)S(1)} %get-tuple-element.105), channel_id=1, source_target_pairs={{0,32},{16,48},{32,0},{48,16},{1,33},{17,49},{33,1},{49,17},{2,34}... | collective-permute-start | bytes 626696 | tf_op jit(solution)/shard_map/ppermute | solution.py:359
  83.3 8.8 %collective-permute-start.19 = (f32[408,128]{1,0:T(8,128)S(1)}, f32[408,128]{1,0:T(8,128)S(1)}, u32[]{:S(2)}, u32[]{:S(2)}) collective-permute-start(f32[408,128]{1,0:T(8,128)S(1)} %get-tuple-element.106), channel_id=1, source_target_pairs={{0,16},{16,0},{32,48},{48,32},{1,17},{17,1},{33,49},{49,33},{2,18}... | collective-permute-start | bytes 626696 | tf_op jit(solution)/shard_map/ppermute | solution.py:359
  83.7 11.3 %collective-permute-start.21 = (f32[408,128]{1,0:T(8,128)S(1)}, f32[408,128]{1,0:T(8,128)S(1)}, u32[]{:S(2)}, u32[]{:S(2)}) collective-permute-start(f32[408,128]{1,0:T(8,128)S(1)} %pad_maximum_fusion.8), channel_id=1, source_target_pairs={{0,48},{16,32},{32,16},{48,0},{1,49},{17,33},{33,17},{49,1},{2,50}... | collective-permute-start | bytes 626696 | tf_op jit(solution)/shard_map/ppermute | solution.py:359
  95.0 5.4 %collective-permute-start.24 = (f32[168,128]{1,0:T(8,128)S(1)}, f32[168,128]{1,0:T(8,128)S(1)}, u32[]{:S(2)}, u32[]{:S(2)}) collective-permute-start(f32[168,128]{1,0:T(8,128)S(1)} %get-tuple-element.102), channel_id=1, source_target_pairs={{0,192},{64,128},{128,64},{192,0},{1,193},{65,129},{129,65},{193,1... | collective-permute-start | bytes 258056 | tf_op jit(solution)/shard_map/ppermute | solution.py:359
  97.2 8.2 %collective-permute-start.23 = (f32[168,128]{1,0:T(8,128)S(1)}, f32[168,128]{1,0:T(8,128)S(1)}, u32[]{:S(2)}, u32[]{:S(2)}) collective-permute-start(f32[168,128]{1,0:T(8,128)S(1)} %get-tuple-element.103), channel_id=1, source_target_pairs={{0,128},{64,192},{128,0},{192,64},{1,129},{65,193},{129,1},{193,65... | collective-permute-start | bytes 258056 | tf_op jit(solution)/shard_map/ppermute | solution.py:359
  97.6 7.8 %collective-permute-start.22 = (f32[168,128]{1,0:T(8,128)S(1)}, f32[168,128]{1,0:T(8,128)S(1)}, u32[]{:S(2)}, u32[]{:S(2)}) collective-permute-start(f32[168,128]{1,0:T(8,128)S(1)} %get-tuple-element.104), channel_id=1, source_target_pairs={{0,64},{64,0},{128,192},{192,128},{1,65},{65,1},{129,193},{193,129... | collective-permute-start | bytes 258056 | tf_op jit(solution)/shard_map/ppermute | solution.py:359
  105.4 4.9 %collective-permute-start.25 = (f32[88,128]{1,0:T(8,128)S(1)}, f32[88,128]{1,0:T(8,128)S(1)}, u32[]{:S(2)}, u32[]{:S(2)}) collective-permute-start(f32[88,128]{1,0:T(8,128)S(1)} %slice.150), channel_id=1, source_target_pairs={{0,193},{1,192},{64,129},{65,128},{128,65},{129,64},{192,1},{193,0... | collective-permute-start | bytes 135176 | tf_op jit(solution)/shard_map/ppermute | solution.py:359
  110.4 4.4 %collective-permute-start.27 = (f32[80,128]{1,0:T(8,128)S(1)}, f32[80,128]{1,0:T(8,128)S(1)}, u32[]{:S(2)}, u32[]{:S(2)}) collective-permute-start(f32[80,128]{1,0:T(8,128)S(1)} %get-tuple-element.101), channel_id=1, source_target_pairs={{0,32},{16,48},{32,0},{48,16},{1,33},{17,49},{33,1},{49,17},{2,34}... | collective-permute-start | bytes 122888 | tf_op jit(solution)/shard_map/ppermute | solution.py:359
  111.8 3.0 %collective-permute-start.26 = (f32[80,128]{1,0:T(8,128)S(1)}, f32[80,128]{1,0:T(8,128)S(1)}, u32[]{:S(2)}, u32[]{:S(2)}) collective-permute-start(f32[80,128]{1,0:T(8,128)S(1)} %get-tuple-element.101), channel_id=1, source_target_pairs={{0,16},{16,0},{32,48},{48,32},{1,17},{17,1},{33,49},{49,33},{2,18}... | collective-permute-start | bytes 122888 | tf_op jit(solution)/shard_map/ppermute | solution.py:359
  111.8 4.1 %collective-permute-start.28 = (f32[80,128]{1,0:T(8,128)S(1)}, f32[80,128]{1,0:T(8,128)S(1)}, u32[]{:S(2)}, u32[]{:S(2)}) collective-permute-start(f32[80,128]{1,0:T(8,128)S(1)} %get-tuple-element.101), channel_id=1, source_target_pairs={{0,48},{16,32},{32,16},{48,0},{1,49},{17,33},{33,17},{49,1},{2,50}... | collective-permute-start | bytes 122888 | tf_op jit(solution)/shard_map/ppermute | solution.py:359
  115.9 6.5 %collective-permute-start.30 = (f32[4,80,128]{2,1,0:T(8,128)S(1)}, f32[4,80,128]{2,1,0:T(8,128)S(1)}, u32[]{:S(2)}, u32[]{:S(2)}) collective-permute-start(f32[4,80,128]{2,1,0:T(8,128)S(1)} %get-tuple-element.94), channel_id=1, source_target_pairs={{0,4},{2,6},{4,0},{6,2},{1,5},{3,7},{5,1},{7,3},{8,12},{10,14},{12... | collective-permute-start | bytes 491528 | tf_op jit(solution)/shard_map/ppermute | solution.py:359
  119.7 4.9 %collective-permute-start.29 = (f32[4,80,128]{2,1,0:T(8,128)S(1)}, f32[4,80,128]{2,1,0:T(8,128)S(1)}, u32[]{:S(2)}, u32[]{:S(2)}) collective-permute-start(f32[4,80,128]{2,1,0:T(8,128)S(1)} %get-tuple-element.94), channel_id=1, source_target_pairs={{0,2},{2,0},{4,6},{6,4},{1,3},{3,1},{5,7},{7,5},{8,10},{10,8},{12,... | collective-permute-start | bytes 491528 | tf_op jit(solution)/shard_map/ppermute | solution.py:359
  120.1 7.1 %collective-permute-start.31 = (f32[4,80,128]{2,1,0:T(8,128)S(1)}, f32[4,80,128]{2,1,0:T(8,128)S(1)}, u32[]{:S(2)}, u32[]{:S(2)}) collective-permute-start(f32[4,80,128]{2,1,0:T(8,128)S(1)} %get-tuple-element.94), channel_id=1, source_target_pairs={{0,6},{2,4},{4,2},{6,0},{1,7},{3,5},{5,3},{7,1},{8,14},{10,12},{12... | collective-permute-start | bytes 491528 | tf_op jit(solution)/shard_map/ppermute | solution.py:359
  127.3 12.7 %collective-permute-start.32 = (f32[4,4,80,128]{3,2,1,0:T(8,128)S(1)}, f32[4,4,80,128]{3,2,1,0:T(8,128)S(1)}, u32[]{:S(2)}, u32[]{:S(2)}) collective-permute-start(f32[4,4,80,128]{3,2,1,0:T(8,128)S(1)} %pad_maximum_fusion.1.source), channel_id=1, source_target_pairs={{0,8},{8,0},{1,9},{9,1},{2,10},{10,2},{3,11},{11,3},{4,12},{12,4},... | collective-permute-start | bytes 1966088 | tf_op jit(solution)/shard_map/ppermute | solution.py:359
where the time goes:
time: 141 us
  waiting for transfers between devices  54.9 us (39%)
  starting transfers between devices  50.2 us (36%)
  Pallas kernels  26.8 us (19%)
  local copies, waits for them, and re-layouts  5.62 us (4%)
  other arithmetic  2.4 us (2%)
    ppermute x33, waiting for transfers between devices, swap(): return lax.ppermute(value, axis, [(i, i ^ mask) for i in range(count)])  54.9 us
    ppermute x33, starting transfers between devices, swap(): return lax.ppermute(value, axis, [(i, i ^ mask) for i in range(count)])  50.2 us
    pallas_call x7, Pallas kernels, call(): pl.pallas_call(kernel, grid_spec=pltpu.PrefetchScalarGridSpec(num_scalar_...  23.7 us
    unnamed x22, local copies, waits for them, and re-layouts  4.18 us
  transfers between devices with their start and end apart: 33, of which 24 were waited for; matrix products, arithmetic and copies ran while one was open for 1% of the time, Pallas kernels for 15%

commit v1 on v0

--- a/solution.py
+++ b/solution.py
@@ -69,23 +69,32 @@
     return jnp.bitwise_and(iota(0, (T, HM)), size) != 0
 
 
-def pick_kernel(owners, states, keep, send, buffer, sems):
+def pick_kernel(owners, states, keep, send, sems):
     core, x, z = lax.axis_index("c"), lax.axis_index("x"), lax.axis_index("z")
     index = (z * 4 + x) * 2 + core
-    copies = [
-        pltpu.make_async_copy(states.at[jnp.bitwise_xor(core, turn)], buffer.at[turn], sems.at[turn])
-        for turn in (0, 1)
-    ]
-    copies[1].start()
-    copies[0].start()
-    for turn, out in ((1, send), (0, keep)):
-        owned = owners[0, jnp.bitwise_xor(core, turn)] == index
-        copies[turn].wait()
+
+    def copies(turn, out):
+        prompt = jnp.bitwise_xor(core, turn)
         for kx in range(4):
             for kz in range(4):
-                row = jnp.bitwise_xor(z, kz) * 16
-                block = buffer[turn, jnp.bitwise_xor(x, kx), pl.ds(pl.multiple_of(row, 16), 16), :]
-                out[kx, kz] = jnp.where(owned, block, 0.0)
+                row = pl.multiple_of(jnp.bitwise_xor(z, kz) * 16, 16)
+                source = states.at[prompt, jnp.bitwise_xor(x, kx), pl.ds(row, 16), :]
+                yield pltpu.make_async_copy(source, out.at[kx, kz], sems.at[turn, kx, kz])
+
+    for step in ("start", "wait"):
+        for turn, out in ((1, send), (0, keep)):
+            owned = owners[0, jnp.bitwise_xor(core, turn)] == index
+
+            @pl.when(owned)
+            def _():
+                for copy in copies(turn, out):
+                    getattr(copy, step)()
+
+            if step == "start":
+
+                @pl.when(jnp.logical_not(owned))
+                def _():
+                    out[...] = jnp.zeros_like(out)
 
 
 def first_kernel(turn, place, adv, hid, q, k, v, og, wg, bias, vec, at, yz):
@@ -411,10 +420,10 @@
         out_shape=(VMEM((4, 4, 16, DH), F32), VMEM((4, 4, 16, DH), F32)),
         in_specs=[whole(SMEM), whole(pl.ANY)],
         out_specs=(whole(), whole()),
-        scratch_shapes=[VMEM((2, 4, 64, DH), F32), pltpu.SemaphoreType.DMA((2,))],
+        scratch_shapes=[pltpu.SemaphoreType.DMA((2, 4, 4))],
         compiler_params=LIMIT,
         name="pick",
-    )(owners, states)
+    )(pltpu.with_memory_space_constraint(owners, pltpu.HBM), pltpu.with_memory_space_constraint(states, pltpu.HBM))
 
     other = swap(send, "c", 1)
     held = keep + other

time: 141 us -> 140 us (level)
  local copies, waits for them, and re-layouts: 5.62 us -> 3.66 us
    unnamed x22 -> x18, local copies, waits for them, and re-layouts: 4.18 us -> 2.21 us
where the time goes in v1:
time: 140 us
  waiting for transfers between devices  55.2 us (39%)
  starting transfers between devices  50.6 us (36%)
  Pallas kernels  26.8 us (19%)
  local copies, waits for them, and re-layouts  3.66 us (3%)
  other arithmetic  2.38 us (2%)
    ppermute x33, waiting for transfers between devices, swap(): return lax.ppermute(value, axis, [(i, i ^ mask) for i in range(count)])  55.2 us
    ppermute x33, starting transfers between devices, swap(): return lax.ppermute(value, axis, [(i, i ^ mask) for i in range(count)])  50.6 us
    pallas_call x7, Pallas kernels, call(): pl.pallas_call(kernel, grid_spec=pltpu.PrefetchScalarGridSpec(num_scalar_...  23.7 us
  transfers between devices with their start and end apart: 33, of which 24 were waited for; matrix products, arithmetic and copies ran while one was open for 1% of the time, Pallas kernels for 15%

profile of v1, /device:TPU:1, one launch (start us, length us, event | category | flops | bytes accessed | tf_op | source)
XLA Modules:
  0.0 139.8 jit_solution(17447461766327226891)
XLA Ops:
  0.6 1.1 pick.1
  1.8 3.3 %collective-permute-start = (f32[4,4,16,640]{3,2,1,0:T(8,128)S(1)}, f32[4,4,16,640]{3,2,1,0:T(8,128)S(1)}, u32[]{:S(2)}, u32[]{:S(2)}) collective-permute-start(f32[4,4,16,640]{3,2,1,0:T(8,128)S(1)} %get-tuple-element.39), channel_id=1, source_target_pairs={{0,8},{8,0},{1,9},{9,1},{2,10},{10,2},{3,11},{11,3},{4,12},{12,4},... | collective-permute-start | bytes 1966088 | tf_op jit(solution)/shard_map/ppermute | solution.py:368
  5.0 1.7 %collective-permute-done = f32[4,4,16,640]{3,2,1,0:T(8,128)S(1)} collective-permute-done((f32[4,4,16,640]{3,2,1,0:T(8,128)S(1)}, f32[4,4,16,640]{3,2,1,0:T(8,128)S(1)}, u32[]{:S(2)}, u32[]{:S(2)}) %collective-permute-start) | collective-permute-done | bytes 655392 | tf_op jit(solution)/shard_map/ppermute | solution.py:368
  6.9 0.9 collective-permute-start.3
  7.8 0.5 collective-permute-start.2
  8.3 2.0 %collective-permute-start.1 = (f32[4,16,640]{2,1,0:T(8,128)S(1)}, f32[4,16,640]{2,1,0:T(8,128)S(1)}, u32[]{:S(2)}, u32[]{:S(2)}) collective-permute-start(f32[4,16,640]{2,1,0:T(8,128)S(1)} %get-tuple-element.86), channel_id=1, source_target_pairs={{0,16},{16,0},{32,48},{48,32},{1,17},{17,1},{33,49},{49,33},{2,18}... | collective-permute-start | bytes 491528 | tf_op jit(solution)/shard_map/ppermute | solution.py:368
  10.2 6.9 %collective-permute-done.3 = f32[4,16,640]{2,1,0:T(8,128)S(1)} collective-permute-done((f32[4,16,640]{2,1,0:T(8,128)S(1)}, f32[4,16,640]{2,1,0:T(8,128)S(1)}, u32[]{:S(2)}, u32[]{:S(2)}) %collective-permute-start.3) | collective-permute-done | bytes 163872 | tf_op jit(solution)/shard_map/ppermute | solution.py:368
  17.6 2.7 %collective-permute-start.6 = (f32[16,640]{1,0:T(8,128)S(1)}, f32[16,640]{1,0:T(8,128)S(1)}, u32[]{:S(2)}, u32[]{:S(2)}) collective-permute-start(f32[16,640]{1,0:T(8,128)S(1)} %get-tuple-element.97), channel_id=1, source_target_pairs={{0,192},{64,128},{128,64},{192,0},{1,193},{65,129},{129,65},{193,1... | collective-permute-start | bytes 122888 | tf_op jit(solution)/shard_map/ppermute | solution.py:368
  20.3 0.9 collective-permute-start.4
  21.2 1.1 collective-permute-done.6
  22.3 2.5 %collective-permute-done.5 = f32[16,640]{1,0:T(8,128)S(1)} collective-permute-done((f32[16,640]{1,0:T(8,128)S(1)}, f32[16,640]{1,0:T(8,128)S(1)}, u32[]{:S(2)}, u32[]{:S(2)}) %collective-permute-start.5) | collective-permute-done | bytes 40992 | tf_op jit(solution)/shard_map/ppermute | solution.py:368
  24.9 1.2 collective-permute-start.9
  26.1 2.4 %collective-permute-start.7 = (f32[16,640]{1,0:T(8,128)S(1)}, f32[16,640]{1,0:T(8,128)S(1)}, u32[]{:S(2)}, u32[]{:S(2)}) collective-permute-start(f32[16,640]{1,0:T(8,128)S(1)} %fusion.11), channel_id=1, source_target_pairs={{0,64},{64,0},{128,192},{192,128},{1,65},{65,1},{129,193},{193,129... | collective-permute-start | bytes 122888 | tf_op jit(solution)/shard_map/ppermute | solution.py:368
  28.5 1.1 collective-permute-done.9
  29.7 1.2 collective-permute-done.8
  30.9 0.7 fusion.13
  31.6 1.7 %collective-permute-start.11 = (f32[4,16,640]{2,1,0:T(8,128)}, f32[4,16,640]{2,1,0:T(8,128)}, u32[]{:S(2)}, u32[]{:S(2)}) collective-permute-start(f32[4,16,640]{2,1,0:T(8,128)} %get-tuple-element.96), channel_id=1, source_target_pairs={{0,32},{16,48},{32,0},{48,16},{1,33},{17,49},{33,1},{49,17},{2,34}... | collective-permute-start | bytes 491528 | tf_op jit(solution)/shard_map/ppermute | solution.py:368
  33.6 1.3 collective-permute-start.12
  34.9 2.7 %collective-permute-done.11 = f32[4,16,640]{2,1,0:T(8,128)} collective-permute-done((f32[4,16,640]{2,1,0:T(8,128)}, f32[4,16,640]{2,1,0:T(8,128)}, u32[]{:S(2)}, u32[]{:S(2)}) %collective-permute-start.11) | collective-permute-done | bytes 163872 | tf_op jit(solution)/shard_map/ppermute | solution.py:368
  37.6 0.8 collective-permute-done.10
  38.3 1.0 collective-permute-done.12
  39.3 1.1 pad_maximum_fusion.anchors
  40.4 6.0 %collective-permute-start.13 = (f32[4,4,16,640]{3,2,1,0:T(8,128)S(1)}, f32[4,4,16,640]{3,2,1,0:T(8,128)S(1)}, u32[]{:S(2)}, u32[]{:S(2)}) collective-permute-start(f32[4,4,16,640]{3,2,1,0:T(8,128)S(1)} %pad_maximum_fusion.anchors), channel_id=1, source_target_pairs={{0,8},{8,0},{1,9},{9,1},{2,10},{10,2},{3,11},{11,3},{4,12},{12,4},... | collective-permute-start | bytes 1966088 | tf_op jit(solution)/shard_map/ppermute | solution.py:368
  46.5 1.1 copy-done.4
  47.5 1.1 copy-done.5
  48.6 4.2 %shard_map.163 = (f32[1,6,128,128]{3,2,1,0:T(8,128)S(1)}, f32[1,256,256]{2,1,0:T(8,128)S(1)}, f32[1,7,128,128]{3,2,1,0:T(8,128)S(1)}) custom-call(s32[8]{0:T(128)S(1)} %concatenate.40.place, f32[2]{0:T(128)S(1)} %bitcast.104, bf16[2,128,2560]{2,1,0:T(8,128)(2,1)S(1)} %bitcast.78, bf16[2,128,1280]{2,1,0:T(8,128)(2,1)S(1)} %bitcast.84, ...), custom_call_target="tpu_custom_call" | custom-call | flops 3000000000 | bytes 3000000 | tf_op jit(solution)/shard_map/pallas_call | solution.py:396
  52.8 4.2 %shard_map.162 = (f32[1,6,128,128]{3,2,1,0:T(8,128)S(1)}, f32[1,256,256]{2,1,0:T(8,128)S(1)}, f32[1,7,128,128]{3,2,1,0:T(8,128)S(1)}) custom-call(s32[8]{0:T(128)S(1)} %concatenate.40.place, f32[2]{0:T(128)S(1)} %bitcast.105, bf16[2,128,2560]{2,1,0:T(8,128)(2,1)S(1)} %bitcast.79, bf16[2,128,1280]{2,1,0:T(8,128)(2,1)S(1)} %bitcast.85, ...), custom_call_target="tpu_custom_call" | custom-call | flops 3000000000 | bytes 3000000 | tf_op jit(solution)/shard_map/pallas_call | solution.py:396
  57.0 3.2 %shard_map.164 = (f32[2,128,128]{2,1,0:T(8,128)S(1)}, bf16[128,128]{1,0:T(8,128)(2,1)S(1)}, bf16[128,640]{1,0:T(8,128)(2,1)S(1)}, f32[2560,128]{1,0:T(8,128)S(1)}, f32[8,128]{1,0:T(8,128)S(1)}) custom-call(s32[8]{0:T(128)S(1)} %concatenate.40.place, f32[2]{0:T(128)S(1)} %bitcast.106, f32[1,6,128,128]{3,2,1,0:T(8,128)S(1)} %get-tuple-element.40.vec.vec_a, ...), custom_call_target="tpu_custom_call" | custom-call | flops 3000000000 | bytes 3000000 | tf_op jit(solution)/shard_map/pallas_call | solution.py:396
  60.2 3.3 %shard_map.165 = (f32[2,128,128]{2,1,0:T(8,128)S(1)}, bf16[128,128]{1,0:T(8,128)(2,1)S(1)}, bf16[128,640]{1,0:T(8,128)(2,1)S(1)}, f32[1288,128]{1,0:T(8,128)S(1)}, f32[1288,128]{1,0:T(8,128)S(1)}) custom-call(s32[8]{0:T(128)S(1)} %concatenate.40.place, f32[2]{0:T(128)S(1)} %bitcast.107, f32[1,6,128,128]{3,2,1,0:T(8,128)S(1)} %get-tuple-element.35.vec.vec_b, ...), custom_call_target="tpu_custom_call" | custom-call | flops 3000000000 | bytes 3000000 | tf_op jit(solution)/shard_map/pallas_call | solution.py:396
  63.9 2.4 %shard_map.168 = (f32[4,4,2,5,8,128]{5,4,3,2,1,0:T(8,128)S(1)}, f32[4,4,2,5,8,128]{5,4,3,2,1,0:T(8,128)S(1)}) custom-call(s32[8]{0:T(128)S(1)} %concatenate.40.place, f32[2]{0:T(128)S(1)} %bitcast.108, f32[1,6,128,128]{3,2,1,0:T(8,128)S(1)} %get-tuple-element.40.vec.vec_a, f32[1,6,128,128]{3,2,1,0:T(8,128)S(1)} %get-tuple-element.35.vec.vec_b, ...), custom_call_target="tpu_custom_call" | custom-call | flops 1000000000 | bytes 3000000 | tf_op jit(solution)/shard_map/pallas_call | solution.py:396
  66.3 0.6 collective-permute-start.18
  66.8 1.7 %collective-permute-done.18 = f32[4,4,2,5,8,128]{5,4,3,2,1,0:T(8,128)S(1)} collective-permute-done((f32[4,4,2,5,8,128]{5,4,3,2,1,0:T(8,128)S(1)}, f32[4,4,2,5,8,128]{5,4,3,2,1,0:T(8,128)S(1)}, u32[]{:S(2)}, u32[]{:S(2)}) %collective-permute-start.18) | collective-permute-done | bytes 655392 | tf_op jit(solution)/shard_map/ppermute | solution.py:368
  68.9 3.0 %collective-permute-start.16 = (f32[328,128]{1,0:T(8,128)S(1)}, f32[328,128]{1,0:T(8,128)S(1)}, u32[]{:S(2)}, u32[]{:S(2)}) collective-permute-start(f32[328,128]{1,0:T(8,128)S(1)} %get-tuple-element.107), channel_id=1, source_target_pairs={{0,4},{2,6},{4,0},{6,2},{1,5},{3,7},{5,1},{7,3},{8,12},{10,14},{12... | collective-permute-start | bytes 503816 | tf_op jit(solution)/shard_map/ppermute | solution.py:368
  71.9 1.1 collective-permute-start.15
  73.0 2.9 %collective-permute-done.16 = f32[328,128]{1,0:T(8,128)S(1)} collective-permute-done((f32[328,128]{1,0:T(8,128)S(1)}, f32[328,128]{1,0:T(8,128)S(1)}, u32[]{:S(2)}, u32[]{:S(2)}) %collective-permute-start.16) | collective-permute-done | bytes 167968 | tf_op jit(solution)/shard_map/ppermute | solution.py:368
  75.9 4.7 %collective-permute-done.15 = f32[328,128]{1,0:T(8,128)S(1)} collective-permute-done((f32[328,128]{1,0:T(8,128)S(1)}, f32[328,128]{1,0:T(8,128)S(1)}, u32[]{:S(2)}, u32[]{:S(2)}) %collective-permute-start.15) | collective-permute-done | bytes 167968 | tf_op jit(solution)/shard_map/ppermute | solution.py:368
  80.7 0.6 collective-permute-start.20
  81.3 1.0 collective-permute-start.19
  82.3 1.8 %collective-permute-start.21 = (f32[408,128]{1,0:T(8,128)S(1)}, f32[408,128]{1,0:T(8,128)S(1)}, u32[]{:S(2)}, u32[]{:S(2)}) collective-permute-start(f32[408,128]{1,0:T(8,128)S(1)} %pad_maximum_fusion.8), channel_id=1, source_target_pairs={{0,48},{16,32},{32,16},{48,0},{1,49},{17,33},{33,17},{49,1},{2,50}... | collective-permute-start | bytes 626696 | tf_op jit(solution)/shard_map/ppermute | solution.py:368
  84.1 3.6 %collective-permute-done.20 = f32[408,128]{1,0:T(8,128)S(1)} collective-permute-done((f32[408,128]{1,0:T(8,128)S(1)}, f32[408,128]{1,0:T(8,128)S(1)}, u32[]{:S(2)}, u32[]{:S(2)}) %collective-permute-start.20) | collective-permute-done | bytes 208928 | tf_op jit(solution)/shard_map/ppermute | solution.py:368
  87.8 3.0 %collective-permute-done.19 = f32[408,128]{1,0:T(8,128)S(1)} collective-permute-done((f32[408,128]{1,0:T(8,128)S(1)}, f32[408,128]{1,0:T(8,128)S(1)}, u32[]{:S(2)}, u32[]{:S(2)}) %collective-permute-start.19) | collective-permute-done | bytes 208928 | tf_op jit(solution)/shard_map/ppermute | solution.py:368
  90.8 2.8 %collective-permute-done.21 = f32[408,128]{1,0:T(8,128)S(1)} collective-permute-done((f32[408,128]{1,0:T(8,128)S(1)}, f32[408,128]{1,0:T(8,128)S(1)}, u32[]{:S(2)}, u32[]{:S(2)}) %collective-permute-start.21) | collective-permute-done | bytes 208928 | tf_op jit(solution)/shard_map/ppermute | solution.py:368
  93.7 2.2 %collective-permute-start.24 = (f32[168,128]{1,0:T(8,128)S(1)}, f32[168,128]{1,0:T(8,128)S(1)}, u32[]{:S(2)}, u32[]{:S(2)}) collective-permute-start(f32[168,128]{1,0:T(8,128)S(1)} %get-tuple-element.102), channel_id=1, source_target_pairs={{0,192},{64,128},{128,64},{192,0},{1,193},{65,129},{129,65},{193,1... | collective-permute-start | bytes 258056 | tf_op jit(solution)/shard_map/ppermute | solution.py:368
  96.3 1.1 collective-permute-start.22
  97.3 1.7 %collective-permute-done.24 = f32[168,128]{1,0:T(8,128)S(1)} collective-permute-done((f32[168,128]{1,0:T(8,128)S(1)}, f32[168,128]{1,0:T(8,128)S(1)}, u32[]{:S(2)}, u32[]{:S(2)}) %collective-permute-start.24) | collective-permute-done | bytes 86048 | tf_op jit(solution)/shard_map/ppermute | solution.py:368
  99.0 5.0 %collective-permute-done.23 = f32[168,128]{1,0:T(8,128)S(1)} collective-permute-done((f32[168,128]{1,0:T(8,128)S(1)}, f32[168,128]{1,0:T(8,128)S(1)}, u32[]{:S(2)}, u32[]{:S(2)}) %collective-permute-start.23) | collective-permute-done | bytes 86048 | tf_op jit(solution)/shard_map/ppermute | solution.py:368
  104.1 3.8 %collective-permute-start.25 = (f32[88,128]{1,0:T(8,128)S(1)}, f32[88,128]{1,0:T(8,128)S(1)}, u32[]{:S(2)}, u32[]{:S(2)}) collective-permute-start(f32[88,128]{1,0:T(8,128)S(1)} %slice.150), channel_id=1, source_target_pairs={{0,193},{1,192},{64,129},{65,128},{128,65},{129,64},{192,1},{193,0... | collective-permute-start | bytes 135176 | tf_op jit(solution)/shard_map/ppermute | solution.py:368
  107.8 1.4 %collective-permute-done.25 = f32[88,128]{1,0:T(8,128)S(1)} collective-permute-done((f32[88,128]{1,0:T(8,128)S(1)}, f32[88,128]{1,0:T(8,128)S(1)}, u32[]{:S(2)}, u32[]{:S(2)}) %collective-permute-start.25) | collective-permute-done | bytes 45088 | tf_op jit(solution)/shard_map/ppermute | solution.py:368
  109.3 0.5 collective-permute-start.27
  109.8 0.6 collective-permute-start.26
  110.4 2.2 %collective-permute-start.28 = (f32[80,128]{1,0:T(8,128)S(1)}, f32[80,128]{1,0:T(8,128)S(1)}, u32[]{:S(2)}, u32[]{:S(2)}) collective-permute-start(f32[80,128]{1,0:T(8,128)S(1)} %get-tuple-element.101), channel_id=1, source_target_pairs={{0,48},{16,32},{32,16},{48,0},{1,49},{17,33},{33,17},{49,1},{2,50}... | collective-permute-start | bytes 122888 | tf_op jit(solution)/shard_map/ppermute | solution.py:368
  112.6 1.1 collective-permute-done.27
  113.7 0.8 collective-permute-done.28
  114.5 3.1 %collective-permute-start.30 = (f32[4,80,128]{2,1,0:T(8,128)S(1)}, f32[4,80,128]{2,1,0:T(8,128)S(1)}, u32[]{:S(2)}, u32[]{:S(2)}) collective-permute-start(f32[4,80,128]{2,1,0:T(8,128)S(1)} %get-tuple-element.94), channel_id=1, source_target_pairs={{0,4},{2,6},{4,0},{6,2},{1,5},{3,7},{5,1},{7,3},{8,12},{10,14},{12... | collective-permute-start | bytes 491528 | tf_op jit(solution)/shard_map/ppermute | solution.py:368
  117.6 0.6 collective-permute-start.29
  118.3 2.1 %collective-permute-done.30 = f32[4,80,128]{2,1,0:T(8,128)S(1)} collective-permute-done((f32[4,80,128]{2,1,0:T(8,128)S(1)}, f32[4,80,128]{2,1,0:T(8,128)S(1)}, u32[]{:S(2)}, u32[]{:S(2)}) %collective-permute-start.30) | collective-permute-done | bytes 163872 | tf_op jit(solution)/shard_map/ppermute | solution.py:368
  120.4 2.3 %collective-permute-done.29 = f32[4,80,128]{2,1,0:T(8,128)S(1)} collective-permute-done((f32[4,80,128]{2,1,0:T(8,128)S(1)}, f32[4,80,128]{2,1,0:T(8,128)S(1)}, u32[]{:S(2)}, u32[]{:S(2)}) %collective-permute-start.29) | collective-permute-done | bytes 163872 | tf_op jit(solution)/shard_map/ppermute | solution.py:368
  122.7 2.7 %collective-permute-done.31 = f32[4,80,128]{2,1,0:T(8,128)S(1)} collective-permute-done((f32[4,80,128]{2,1,0:T(8,128)S(1)}, f32[4,80,128]{2,1,0:T(8,128)S(1)}, u32[]{:S(2)}, u32[]{:S(2)}) %collective-permute-start.31) | collective-permute-done | bytes 163872 | tf_op jit(solution)/shard_map/ppermute | solution.py:368
  125.4 4.6 %collective-permute-start.32 = (f32[4,4,80,128]{3,2,1,0:T(8,128)S(1)}, f32[4,4,80,128]{3,2,1,0:T(8,128)S(1)}, u32[]{:S(2)}, u32[]{:S(2)}) collective-permute-start(f32[4,4,80,128]{3,2,1,0:T(8,128)S(1)} %pad_maximum_fusion.1.source), channel_id=1, source_target_pairs={{0,8},{8,0},{1,9},{9,1},{2,10},{10,2},{3,11},{11,3},{4,12},{12,4},... | collective-permute-start | bytes 1966088 | tf_op jit(solution)/shard_map/ppermute | solution.py:368
  130.0 3.2 %shard_map.166 = (bf16[2,128,1280]{2,1,0:T(8,128)(2,1)}, bf16[2,128,1280]{2,1,0:T(8,128)(2,1)}, bf16[2,128,1280]{2,1,0:T(8,128)(2,1)}, bf16[2,128,2560]{2,1,0:T(8,128)(2,1)}) custom-call(s32[8]{0:T(128)S(1)} %concatenate.40.place, f32[2]{0:T(128)S(1)} %bitcast.109, f32[1,6,128,128]{3,2,1,0:T(8,128)S(1)} %get-tuple-element.40.vec.vec_a, ...), custom_call_target="tpu_custom_call" | custom-call | flops 3000000000 | bytes 3000000 | tf_op jit(solution)/shard_map/pallas_call | solution.py:396
  133.2 3.2 %shard_map.167 = (bf16[2,128,1280]{2,1,0:T(8,128)(2,1)}, bf16[2,128,1280]{2,1,0:T(8,128)(2,1)}, bf16[2,128,1280]{2,1,0:T(8,128)(2,1)}, bf16[2,128,2560]{2,1,0:T(8,128)(2,1)}) custom-call(s32[8]{0:T(128)S(1)} %concatenate.40.place, f32[2]{0:T(128)S(1)} %bitcast.110, ...), custom_call_target="tpu_custom_call", output_to_operand_aliasing={{0}: (11, {}), {1}: (12, {}), {2}: (13, {}), {3}: (14, {})} | custom-call | flops 3000000000 | bytes 3000000 | tf_op jit(solution)/shard_map/pallas_call | solution.py:396
  136.5 0.6 broadcast_in_dim_reshape.3
  137.6 1.0 shard_map.169.refs_0_
  138.6 1.0 shard_map.170
  (66 shorter events, 3.0 us)
Async XLA Ops:
  1.8 5.0 %collective-permute-start = (f32[4,4,16,640]{3,2,1,0:T(8,128)S(1)}, f32[4,4,16,640]{3,2,1,0:T(8,128)S(1)}, u32[]{:S(2)}, u32[]{:S(2)}) collective-permute-start(f32[4,4,16,640]{3,2,1,0:T(8,128)S(1)} %get-tuple-element.39), channel_id=1, source_target_pairs={{0,8},{8,0},{1,9},{9,1},{2,10},{10,2},{3,11},{11,3},{4,12},{12,4},... | collective-permute-start | bytes 1966088 | tf_op jit(solution)/shard_map/ppermute | solution.py:368
  6.8 28.0 %copy-start.8 = (s32[1,2,1]{1,2,0:T(1,128)S(1)}, s32[1,2,1]{1,2,0:T(1,128)}, u32[]{:S(2)}) copy-start(s32[1,2,1]{1,2,0:T(1,128)} %param.20) | copy-start | bytes 28
  6.9 39.6 %copy-start.3 = (bf16[1,2,1,128,1280]{4,3,2,1,0:T(8,128)(2,1)S(1)}, bf16[1,2,1,128,1280]{4,3,2,1,0:T(8,128)(2,1)}, u32[]{:S(2)}) copy-start(bf16[1,2,1,128,1280]{4,3,2,1,0:T(8,128)(2,1)} %param.13) | copy-start | bytes 1966084
  6.9 10.2 %collective-permute-start.3 = (f32[4,16,640]{2,1,0:T(8,128)S(1)}, f32[4,16,640]{2,1,0:T(8,128)S(1)}, u32[]{:S(2)}, u32[]{:S(2)}) collective-permute-start(f32[4,16,640]{2,1,0:T(8,128)S(1)} %get-tuple-element.84), channel_id=1, source_target_pairs={{0,48},{16,32},{32,16},{48,0},{1,49},{17,33},{33,17},{49,1},{2,50}... | collective-permute-start | bytes 491528 | tf_op jit(solution)/shard_map/ppermute | solution.py:368
  7.8 9.3 %collective-permute-start.2 = (f32[4,16,640]{2,1,0:T(8,128)S(1)}, f32[4,16,640]{2,1,0:T(8,128)S(1)}, u32[]{:S(2)}, u32[]{:S(2)}) collective-permute-start(f32[4,16,640]{2,1,0:T(8,128)S(1)} %get-tuple-element.85), channel_id=1, source_target_pairs={{0,32},{16,48},{32,0},{48,16},{1,33},{17,49},{33,1},{49,17},{2,34}... | collective-permute-start | bytes 491528 | tf_op jit(solution)/shard_map/ppermute | solution.py:368
  8.3 9.2 %collective-permute-start.1 = (f32[4,16,640]{2,1,0:T(8,128)S(1)}, f32[4,16,640]{2,1,0:T(8,128)S(1)}, u32[]{:S(2)}, u32[]{:S(2)}) collective-permute-start(f32[4,16,640]{2,1,0:T(8,128)S(1)} %get-tuple-element.86), channel_id=1, source_target_pairs={{0,16},{16,0},{32,48},{48,32},{1,17},{17,1},{33,49},{49,33},{2,18}... | collective-permute-start | bytes 491528 | tf_op jit(solution)/shard_map/ppermute | solution.py:368
  17.5 28.9 %copy-start.2 = (bf16[1,2,1,128,1280]{4,3,2,1,0:T(8,128)(2,1)S(1)}, bf16[1,2,1,128,1280]{4,3,2,1,0:T(8,128)(2,1)}, u32[]{:S(2)}) copy-start(bf16[1,2,1,128,1280]{4,3,2,1,0:T(8,128)(2,1)} %param.12) | copy-start | bytes 1966084
  17.5 28.9 %copy-start = (bf16[1,2,1,128,2560]{4,3,2,1,0:T(8,128)(2,1)S(1)}, bf16[1,2,1,128,2560]{4,3,2,1,0:T(8,128)(2,1)}, u32[]{:S(2)}) copy-start(bf16[1,2,1,128,2560]{4,3,2,1,0:T(8,128)(2,1)} %param.11) | copy-start | bytes 3932164
  17.5 28.9 %copy-start.1 = (bf16[1,2,1,128,1280]{4,3,2,1,0:T(8,128)(2,1)S(1)}, bf16[1,2,1,128,1280]{4,3,2,1,0:T(8,128)(2,1)}, u32[]{:S(2)}) copy-start(bf16[1,2,1,128,1280]{4,3,2,1,0:T(8,128)(2,1)} %param.14) | copy-start | bytes 1966084
  17.6 28.9 %copy-start.6 = (f32[128]{0:T(128)S(1)}, f32[128]{0:T(128)}, u32[]{:S(2)}) copy-start(f32[128]{0:T(128)} %param.17) | copy-start | bytes 1540
  17.6 28.9 %copy-start.7 = (f32[1,2,1]{1,2,0:T(1,128)S(1)}, f32[1,2,1]{1,2,0:T(1,128)}, u32[]{:S(2)}) copy-start(f32[1,2,1]{1,2,0:T(1,128)} %param.21) | copy-start | bytes 28
  17.6 4.7 %collective-permute-start.6 = (f32[16,640]{1,0:T(8,128)S(1)}, f32[16,640]{1,0:T(8,128)S(1)}, u32[]{:S(2)}, u32[]{:S(2)}) collective-permute-start(f32[16,640]{1,0:T(8,128)S(1)} %get-tuple-element.97), channel_id=1, source_target_pairs={{0,192},{64,128},{128,64},{192,0},{1,193},{65,129},{129,65},{193,1... | collective-permute-start | bytes 122888 | tf_op jit(solution)/shard_map/ppermute | solution.py:368
  20.3 4.5 %collective-permute-start.5 = (f32[16,640]{1,0:T(8,128)S(1)}, f32[16,640]{1,0:T(8,128)S(1)}, u32[]{:S(2)}, u32[]{:S(2)}) collective-permute-start(f32[16,640]{1,0:T(8,128)S(1)} %get-tuple-element.98), channel_id=1, source_target_pairs={{0,128},{64,192},{128,0},{192,64},{1,129},{65,193},{129,1},{193,65... | collective-permute-start | bytes 122888 | tf_op jit(solution)/shard_map/ppermute | solution.py:368
  20.3 4.5 %collective-permute-start.4 = (f32[16,640]{1,0:T(8,128)S(1)}, f32[16,640]{1,0:T(8,128)S(1)}, u32[]{:S(2)}, u32[]{:S(2)}) collective-permute-start(f32[16,640]{1,0:T(8,128)S(1)} %get-tuple-element.99), channel_id=1, source_target_pairs={{0,64},{64,0},{128,192},{192,128},{1,65},{65,1},{129,193},{193,129... | collective-permute-start | bytes 122888 | tf_op jit(solution)/shard_map/ppermute | solution.py:368
  24.9 4.8 %collective-permute-start.9 = (f32[16,640]{1,0:T(8,128)S(1)}, f32[16,640]{1,0:T(8,128)S(1)}, u32[]{:S(2)}, u32[]{:S(2)}) collective-permute-start(f32[16,640]{1,0:T(8,128)S(1)} %fusion.11), channel_id=1, source_target_pairs={{0,192},{64,128},{128,64},{192,0},{1,193},{65,129},{129,65},{193,1... | collective-permute-start | bytes 122888 | tf_op jit(solution)/shard_map/ppermute | solution.py:368
  26.1 4.8 %collective-permute-start.8 = (f32[16,640]{1,0:T(8,128)S(1)}, f32[16,640]{1,0:T(8,128)S(1)}, u32[]{:S(2)}, u32[]{:S(2)}) collective-permute-start(f32[16,640]{1,0:T(8,128)S(1)} %fusion.11), channel_id=1, source_target_pairs={{0,128},{64,192},{128,0},{192,64},{1,129},{65,193},{129,1},{193,65... | collective-permute-start | bytes 122888 | tf_op jit(solution)/shard_map/ppermute | solution.py:368
  26.1 4.8 %collective-permute-start.7 = (f32[16,640]{1,0:T(8,128)S(1)}, f32[16,640]{1,0:T(8,128)S(1)}, u32[]{:S(2)}, u32[]{:S(2)}) collective-permute-start(f32[16,640]{1,0:T(8,128)S(1)} %fusion.11), channel_id=1, source_target_pairs={{0,64},{64,0},{128,192},{192,128},{1,65},{65,1},{129,193},{193,129... | collective-permute-start | bytes 122888 | tf_op jit(solution)/shard_map/ppermute | solution.py:368
  31.6 6.0 %collective-permute-start.11 = (f32[4,16,640]{2,1,0:T(8,128)}, f32[4,16,640]{2,1,0:T(8,128)}, u32[]{:S(2)}, u32[]{:S(2)}) collective-permute-start(f32[4,16,640]{2,1,0:T(8,128)} %get-tuple-element.96), channel_id=1, source_target_pairs={{0,32},{16,48},{32,0},{48,16},{1,33},{17,49},{33,1},{49,17},{2,34}... | collective-permute-start | bytes 491528 | tf_op jit(solution)/shard_map/ppermute | solution.py:368
  33.2 5.1 %collective-permute-start.10 = (f32[4,16,640]{2,1,0:T(8,128)}, f32[4,16,640]{2,1,0:T(8,128)}, u32[]{:S(2)}, u32[]{:S(2)}) collective-permute-start(f32[4,16,640]{2,1,0:T(8,128)} %get-tuple-element.96), channel_id=1, source_target_pairs={{0,16},{16,0},{32,48},{48,32},{1,17},{17,1},{33,49},{49,33},{2,18}... | collective-permute-start | bytes 491528 | tf_op jit(solution)/shard_map/ppermute | solution.py:368
  33.6 5.8 %collective-permute-start.12 = (f32[4,16,640]{2,1,0:T(8,128)}, f32[4,16,640]{2,1,0:T(8,128)}, u32[]{:S(2)}, u32[]{:S(2)}) collective-permute-start(f32[4,16,640]{2,1,0:T(8,128)} %get-tuple-element.96), channel_id=1, source_target_pairs={{0,48},{16,32},{32,16},{48,0},{1,49},{17,33},{33,17},{49,1},{2,50}... | collective-permute-start | bytes 491528 | tf_op jit(solution)/shard_map/ppermute | solution.py:368
  40.4 19.8 %collective-permute-start.13 = (f32[4,4,16,640]{3,2,1,0:T(8,128)S(1)}, f32[4,4,16,640]{3,2,1,0:T(8,128)S(1)}, u32[]{:S(2)}, u32[]{:S(2)}) collective-permute-start(f32[4,4,16,640]{3,2,1,0:T(8,128)S(1)} %pad_maximum_fusion.anchors), channel_id=1, source_target_pairs={{0,8},{8,0},{1,9},{9,1},{2,10},{10,2},{3,11},{11,3},{4,12},{12,4},... | collective-permute-start | bytes 1966088 | tf_op jit(solution)/shard_map/ppermute | solution.py:368
  46.5 1.1 copy-start.4
  47.5 1.1 copy-start.5
  63.5 5.1 %collective-permute-start.14 = (f32[1288,128]{1,0:T(8,128)S(1)}, f32[1288,128]{1,0:T(8,128)S(1)}, u32[]{:S(2)}, u32[]{:S(2)}) collective-permute-start(f32[1288,128]{1,0:T(8,128)S(1)} %get-tuple-element.60), channel_id=1, source_target_pairs={{0,8},{8,0},{1,9},{9,1},{2,10},{10,2},{3,11},{11,3},{4,12},{12,4},... | collective-permute-start | bytes 1978376 | tf_op jit(solution)/shard_map/ppermute | solution.py:368
  66.3 2.3 %collective-permute-start.18 = (f32[4,4,2,5,8,128]{5,4,3,2,1,0:T(8,128)S(1)}, f32[4,4,2,5,8,128]{5,4,3,2,1,0:T(8,128)S(1)}, u32[]{:S(2)}, u32[]{:S(2)}) collective-permute-start(f32[4,4,2,5,8,128]{5,4,3,2,1,0:T(8,128)S(1)} %get-tuple-element.62), channel_id=1, source_target_pairs={{0,8},{8,0},{1,9},{9,1},{2,10},{10,2},{3,11},{11,3},{4,12},{12,4},... | collective-permute-start | bytes 1966088 | tf_op jit(solution)/shard_map/ppermute | solution.py:368
  68.9 7.1 %collective-permute-start.16 = (f32[328,128]{1,0:T(8,128)S(1)}, f32[328,128]{1,0:T(8,128)S(1)}, u32[]{:S(2)}, u32[]{:S(2)}) collective-permute-start(f32[328,128]{1,0:T(8,128)S(1)} %get-tuple-element.107), channel_id=1, source_target_pairs={{0,4},{2,6},{4,0},{6,2},{1,5},{3,7},{5,1},{7,3},{8,12},{10,14},{12... | collective-permute-start | bytes 503816 | tf_op jit(solution)/shard_map/ppermute | solution.py:368
  71.9 8.7 %collective-permute-start.15 = (f32[328,128]{1,0:T(8,128)S(1)}, f32[328,128]{1,0:T(8,128)S(1)}, u32[]{:S(2)}, u32[]{:S(2)}) collective-permute-start(f32[328,128]{1,0:T(8,128)S(1)} %get-tuple-element.108), channel_id=1, source_target_pairs={{0,2},{2,0},{4,6},{6,4},{1,3},{3,1},{5,7},{7,5},{8,10},{10,8},{12,... | collective-permute-start | bytes 503816 | tf_op jit(solution)/shard_map/ppermute | solution.py:368
  72.9 7.7 %collective-permute-start.17 = (f32[328,128]{1,0:T(8,128)S(1)}, f32[328,128]{1,0:T(8,128)S(1)}, u32[]{:S(2)}, u32[]{:S(2)}) collective-permute-start(f32[328,128]{1,0:T(8,128)S(1)} %concatenate.53), channel_id=1, source_target_pairs={{0,6},{2,4},{4,2},{6,0},{1,7},{3,5},{5,3},{7,1},{8,14},{10,12},{12... | collective-permute-start | bytes 503816 | tf_op jit(solution)/shard_map/ppermute | solution.py:368
  80.7 7.1 %collective-permute-start.20 = (f32[408,128]{1,0:T(8,128)S(1)}, f32[408,128]{1,0:T(8,128)S(1)}, u32[]{:S(2)}, u32[]{:S(2)}) collective-permute-start(f32[408,128]{1,0:T(8,128)S(1)} %get-tuple-element.105), channel_id=1, source_target_pairs={{0,32},{16,48},{32,0},{48,16},{1,33},{17,49},{33,1},{49,17},{2,34}... | collective-permute-start | bytes 626696 | tf_op jit(solution)/shard_map/ppermute | solution.py:368
  81.3 9.5 %collective-permute-start.19 = (f32[408,128]{1,0:T(8,128)S(1)}, f32[408,128]{1,0:T(8,128)S(1)}, u32[]{:S(2)}, u32[]{:S(2)}) collective-permute-start(f32[408,128]{1,0:T(8,128)S(1)} %get-tuple-element.106), channel_id=1, source_target_pairs={{0,16},{16,0},{32,48},{48,32},{1,17},{17,1},{33,49},{49,33},{2,18}... | collective-permute-start | bytes 626696 | tf_op jit(solution)/shard_map/ppermute | solution.py:368
  82.3 11.3 %collective-permute-start.21 = (f32[408,128]{1,0:T(8,128)S(1)}, f32[408,128]{1,0:T(8,128)S(1)}, u32[]{:S(2)}, u32[]{:S(2)}) collective-permute-start(f32[408,128]{1,0:T(8,128)S(1)} %pad_maximum_fusion.8), channel_id=1, source_target_pairs={{0,48},{16,32},{32,16},{48,0},{1,49},{17,33},{33,17},{49,1},{2,50}... | collective-permute-start | bytes 626696 | tf_op jit(solution)/shard_map/ppermute | solution.py:368
  93.7 5.4 %collective-permute-start.24 = (f32[168,128]{1,0:T(8,128)S(1)}, f32[168,128]{1,0:T(8,128)S(1)}, u32[]{:S(2)}, u32[]{:S(2)}) collective-permute-start(f32[168,128]{1,0:T(8,128)S(1)} %get-tuple-element.102), channel_id=1, source_target_pairs={{0,192},{64,128},{128,64},{192,0},{1,193},{65,129},{129,65},{193,1... | collective-permute-start | bytes 258056 | tf_op jit(solution)/shard_map/ppermute | solution.py:368
  95.9 8.2 %collective-permute-start.23 = (f32[168,128]{1,0:T(8,128)S(1)}, f32[168,128]{1,0:T(8,128)S(1)}, u32[]{:S(2)}, u32[]{:S(2)}) collective-permute-start(f32[168,128]{1,0:T(8,128)S(1)} %get-tuple-element.103), channel_id=1, source_target_pairs={{0,128},{64,192},{128,0},{192,64},{1,129},{65,193},{129,1},{193,65... | collective-permute-start | bytes 258056 | tf_op jit(solution)/shard_map/ppermute | solution.py:368
  96.3 7.8 %collective-permute-start.22 = (f32[168,128]{1,0:T(8,128)S(1)}, f32[168,128]{1,0:T(8,128)S(1)}, u32[]{:S(2)}, u32[]{:S(2)}) collective-permute-start(f32[168,128]{1,0:T(8,128)S(1)} %get-tuple-element.104), channel_id=1, source_target_pairs={{0,64},{64,0},{128,192},{192,128},{1,65},{65,1},{129,193},{193,129... | collective-permute-start | bytes 258056 | tf_op jit(solution)/shard_map/ppermute | solution.py:368
  104.1 5.2 %collective-permute-start.25 = (f32[88,128]{1,0:T(8,128)S(1)}, f32[88,128]{1,0:T(8,128)S(1)}, u32[]{:S(2)}, u32[]{:S(2)}) collective-permute-start(f32[88,128]{1,0:T(8,128)S(1)} %slice.150), channel_id=1, source_target_pairs={{0,193},{1,192},{64,129},{65,128},{128,65},{129,64},{192,1},{193,0... | collective-permute-start | bytes 135176 | tf_op jit(solution)/shard_map/ppermute | solution.py:368
  109.3 4.4 %collective-permute-start.27 = (f32[80,128]{1,0:T(8,128)S(1)}, f32[80,128]{1,0:T(8,128)S(1)}, u32[]{:S(2)}, u32[]{:S(2)}) collective-permute-start(f32[80,128]{1,0:T(8,128)S(1)} %get-tuple-element.101), channel_id=1, source_target_pairs={{0,32},{16,48},{32,0},{48,16},{1,33},{17,49},{33,1},{49,17},{2,34}... | collective-permute-start | bytes 122888 | tf_op jit(solution)/shard_map/ppermute | solution.py:368
  109.8 3.9 %collective-permute-start.26 = (f32[80,128]{1,0:T(8,128)S(1)}, f32[80,128]{1,0:T(8,128)S(1)}, u32[]{:S(2)}, u32[]{:S(2)}) collective-permute-start(f32[80,128]{1,0:T(8,128)S(1)} %get-tuple-element.101), channel_id=1, source_target_pairs={{0,16},{16,0},{32,48},{48,32},{1,17},{17,1},{33,49},{49,33},{2,18}... | collective-permute-start | bytes 122888 | tf_op jit(solution)/shard_map/ppermute | solution.py:368
  110.4 4.1 %collective-permute-start.28 = (f32[80,128]{1,0:T(8,128)S(1)}, f32[80,128]{1,0:T(8,128)S(1)}, u32[]{:S(2)}, u32[]{:S(2)}) collective-permute-start(f32[80,128]{1,0:T(8,128)S(1)} %get-tuple-element.101), channel_id=1, source_target_pairs={{0,48},{16,32},{32,16},{48,0},{1,49},{17,33},{33,17},{49,1},{2,50}... | collective-permute-start | bytes 122888 | tf_op jit(solution)/shard_map/ppermute | solution.py:368
  114.5 5.8 %collective-permute-start.30 = (f32[4,80,128]{2,1,0:T(8,128)S(1)}, f32[4,80,128]{2,1,0:T(8,128)S(1)}, u32[]{:S(2)}, u32[]{:S(2)}) collective-permute-start(f32[4,80,128]{2,1,0:T(8,128)S(1)} %get-tuple-element.94), channel_id=1, source_target_pairs={{0,4},{2,6},{4,0},{6,2},{1,5},{3,7},{5,1},{7,3},{8,12},{10,14},{12... | collective-permute-start | bytes 491528 | tf_op jit(solution)/shard_map/ppermute | solution.py:368
  117.6 5.0 %collective-permute-start.29 = (f32[4,80,128]{2,1,0:T(8,128)S(1)}, f32[4,80,128]{2,1,0:T(8,128)S(1)}, u32[]{:S(2)}, u32[]{:S(2)}) collective-permute-start(f32[4,80,128]{2,1,0:T(8,128)S(1)} %get-tuple-element.94), channel_id=1, source_target_pairs={{0,2},{2,0},{4,6},{6,4},{1,3},{3,1},{5,7},{7,5},{8,10},{10,8},{12,... | collective-permute-start | bytes 491528 | tf_op jit(solution)/shard_map/ppermute | solution.py:368
  118.2 7.1 %collective-permute-start.31 = (f32[4,80,128]{2,1,0:T(8,128)S(1)}, f32[4,80,128]{2,1,0:T(8,128)S(1)}, u32[]{:S(2)}, u32[]{:S(2)}) collective-permute-start(f32[4,80,128]{2,1,0:T(8,128)S(1)} %get-tuple-element.94), channel_id=1, source_target_pairs={{0,6},{2,4},{4,2},{6,0},{1,7},{3,5},{5,3},{7,1},{8,14},{10,12},{12... | collective-permute-start | bytes 491528 | tf_op jit(solution)/shard_map/ppermute | solution.py:368
  125.4 13.2 %collective-permute-start.32 = (f32[4,4,80,128]{3,2,1,0:T(8,128)S(1)}, f32[4,4,80,128]{3,2,1,0:T(8,128)S(1)}, u32[]{:S(2)}, u32[]{:S(2)}) collective-permute-start(f32[4,4,80,128]{3,2,1,0:T(8,128)S(1)} %pad_maximum_fusion.1.source), channel_id=1, source_target_pairs={{0,8},{8,0},{1,9},{9,1},{2,10},{10,2},{3,11},{11,3},{4,12},{12,4},... | collective-permute-start | bytes 1966088 | tf_op jit(solution)/shard_map/ppermute | solution.py:368
